TPU v7x, 128 devices: a whole 4x4x4 slice. The times are simulated.
128 devices in a mesh: seq: 32 (over x, z, core), head: 4 (over y).
Axes of the slice: x: 4, y: 4, z: 4, core: 2. Of those that a mesh axis runs over, the one named last changes fastest.
Arguments:
- tokens: bfloat16 [2, 16384, 2560], P(None, 'seq'), may hold values from -6 to 6
- gate_weight: bfloat16 [2560, 5120], P(None, 'head'), may hold values from -0.125 to 0.125
- value_weight: bfloat16 [2560, 5120], P(None, 'head'), may hold values from -0.125 to 0.125
- state_weight: bfloat16 [2560, 256], replicated, may hold values from -0.125 to 0.125
- step_weight: bfloat16 [2560, 80], P(None, 'head'), may hold values from -0.125 to 0.125
- value_kernel: float32 [4, 5120], P(None, 'head'), may hold values from -3 to 3
- value_offset: float32 [5120], P('head'), may hold values from -3 to 3
- state_kernel: float32 [4, 256], replicated, may hold values from -3 to 3
- state_offset: float32 [256], replicated, may hold values from -3 to 3
- step_offset: float32 [80], P('head'), may hold values from -2 to 0.5
- decay_rate: float32 [80], P('head'), may hold values from 6.1035156e-05 to 0.1
- skip_gain: float32 [80], P('head'), may hold values from 0.5 to 2
- norm_gain: float32 [5120], P('head'), may hold values from 0.5 to 1.5
Outputs:
- normed: bfloat16 [2, 16384, 5120], P(None, 'seq', 'head')
All inputs are finite; a program needn't handle non-finite values.
Results may differ from a plain program's by a relative error of at most 0.0054.
Values may be sent and summed in bfloat16 or wider, within the bound.
A program may use at most 128 MiB of HBM per device.

v0:
```python
import jax
import jax.numpy as jnp
from jax import lax
from jax.sharding import Mesh
from jax.sharding import PartitionSpec as P

GROUP = 256
INNER = 5120
SEQ = ("seq_0", "seq_1", "seq_2")


EPS = 1e-05


def shifted(value, axis, steps):
    count = lax.axis_size(axis)
    leading, last = (max(0, -steps), min(count, count - steps))
    return lax.ppermute(value, axis, [(source, source + steps) for source in range(leading, last)])


def split_up(array, dim, count):
    before, after = (array.shape[:dim], array.shape[dim + 1 :])
    return jnp.moveaxis(array.reshape(*before, count, -1, *after), dim, 0)


def laid_out(pieces, dim):
    pieces = jnp.moveaxis(pieces, 0, dim)
    shape = pieces.shape
    return pieces.reshape(*shape[:dim], shape[dim] * shape[dim + 1], *shape[dim + 2 :])


def turned_blocks(pieces, axes, order):
    inside = pieces.shape[1:]
    out = pieces.reshape(*(lax.axis_size(a) for a in axes), *inside)
    for k in order:
        out = lax.all_to_all(out, axes[k], k, k, tiled=True)
    return out.reshape(-1, *inside)


def core_and_chips(array, groups, order, split_dim, concat_dim):
    count = lax.axis_size(groups[0]) * lax.axis_size(groups[1])
    pieces = split_up(array, split_dim, count)
    return laid_out(turned_blocks(pieces, groups, order), concat_dim)


def copy_for_each(array, axis):
    count = lax.axis_size(axis)
    return lax.all_to_all(
        jnp.broadcast_to(array[None], (count, *array.shape)), axis, 0, 0, tiled=True
    )


def collect(array, axis, dim):
    pieces = copy_for_each(array, axis)
    return laid_out(pieces, dim)


def of_everyone(array, axis):
    everything = copy_for_each(array, axis)
    return jnp.sum(everything, axis=0)


def conv_rows(previous, incoming, kernel, offset):
    joined = jnp.concatenate([previous, incoming], axis=1).astype(jnp.float32)
    length = incoming.shape[1]
    summed = offset + kernel[0] * lax.slice_in_dim(joined, 0, length, axis=1)
    for tap_index in range(1, kernel.shape[0]):
        summed = summed + kernel[tap_index] * lax.slice_in_dim(
            joined, tap_index, tap_index + length, axis=1
        )
    return jax.nn.silu(summed).astype(jnp.bfloat16)


def local(
    tokens,
    gate_weight,
    value_weight,
    state_weight,
    step_weight,
    value_kernel,
    value_offset,
    state_kernel,
    state_offset,
    step_offset,
    decay_rate,
    skip_gain,
    norm_gain,
):
    batch_count, local_rows, model_width = tokens.shape
    local_inner = gate_weight.shape[1]
    local_heads = step_weight.shape[1]
    head_width = local_inner // local_heads
    state_width = state_weight.shape[1] // 2
    rim_rows = value_kernel.shape[0] - 1
    blocks = local_rows // GROUP
    gate_part = jnp.einsum(
        "btd,dc->btc", tokens, gate_weight, preferred_element_type=jnp.float32
    ).astype(jnp.bfloat16)
    values = jnp.einsum(
        "btd,dc->btc", tokens, value_weight, preferred_element_type=jnp.float32
    ).astype(jnp.bfloat16)
    inout_rows = jnp.einsum(
        "btd,dn->btn", tokens, state_weight, preferred_element_type=jnp.float32
    ).astype(jnp.bfloat16)
    step_sizes = jax.nn.softplus(
        jnp.einsum("btd,dh->bth", tokens, step_weight, preferred_element_type=jnp.float32)
        + step_offset
    )
    edge_rows = jnp.concatenate(
        [values[:, local_rows - rim_rows :], inout_rows[:, local_rows - rim_rows :]], axis=2
    )
    before = shifted(edge_rows, SEQ, 1)
    value_conv = conv_rows(before[:, :, :local_inner], values, value_kernel, value_offset)
    inout_conv = conv_rows(before[:, :, local_inner:], inout_rows, state_kernel, state_offset)
    b_all = inout_conv[:, :, :state_width]
    c_all = inout_conv[:, :, state_width:]
    log_decay = -step_sizes * decay_rate
    cumulative = jnp.cumsum(
        log_decay.reshape(batch_count, blocks, GROUP, local_heads), axis=2
    ).reshape(batch_count, local_rows, local_heads)
    causal = (jnp.arange(GROUP)[:, None] >= jnp.arange(GROUP)[None, :])[None, :, :, None]
    within_list = []
    local_list = []
    before_list = []
    c_list = []
    memory = jnp.zeros((batch_count, local_heads, head_width, state_width), jnp.float32)
    factor = jnp.ones((batch_count, local_heads), jnp.float32)
    log_total = jnp.zeros((batch_count, local_heads), jnp.float32)
    for block_index in range(blocks):
        lower = block_index * GROUP
        upper = lower + GROUP
        cum_block = cumulative[:, lower:upper]
        step_block = step_sizes[:, lower:upper]
        b_block = b_all[:, lower:upper]
        c_block = c_all[:, lower:upper]
        value_block = value_conv[:, lower:upper].reshape(
            batch_count, GROUP, local_heads, head_width
        )
        scores = jnp.einsum("btn,bsn->bts", c_block, b_block, preferred_element_type=jnp.float32)
        spread = jnp.where(causal, cum_block[:, :, None, :] - cum_block[:, None, :, :], 0.0)
        mixing = jnp.where(
            causal, scores[:, :, :, None] * jnp.exp(spread) * step_block[:, None, :, :], 0.0
        ).astype(jnp.bfloat16)
        within_list.append(
            jnp.einsum("btsh,bshp->bthp", mixing, value_block, preferred_element_type=jnp.float32)
        )
        closing = jnp.exp(cum_block[:, -1:] - cum_block) * step_block
        weighted = (closing[:, :, :, None] * b_block.astype(jnp.float32)[:, :, None, :]).astype(
            jnp.bfloat16
        )
        produced = jnp.einsum(
            "bshp,bshn->bhpn", value_block, weighted, preferred_element_type=jnp.float32
        )
        local_list.append(memory)
        before_list.append(factor)
        c_list.append(c_block.astype(jnp.float32))
        through = jnp.exp(cum_block[:, -1])
        memory = through[:, :, None, None] * memory + produced
        factor = factor * through
        log_total = log_total + cum_block[:, -1]
    flat_state = memory.reshape(batch_count, local_heads, head_width * state_width)[None]
    shares = core_and_chips(flat_state, (("seq_0", "seq_1"), "seq_2"), (1, 0), 3, 0)
    logs = collect(log_total[None], SEQ, 0)
    inclusive = jnp.cumsum(logs, axis=0)
    exclusive = inclusive - logs
    peers = logs.shape[0]
    earlier_mask = (jnp.arange(peers)[:, None] > jnp.arange(peers)[None, :])[:, :, None, None]
    spread = jnp.where(earlier_mask, exclusive[:, None] - inclusive[None, :], 0.0)
    weights = jnp.where(earlier_mask, jnp.exp(spread), 0.0)
    prefix_shares = jnp.einsum("jibh,ibhs->jbhs", weights, shares, precision=lax.Precision.HIGHEST)
    returned = lax.all_to_all(prefix_shares, SEQ, split_axis=0, concat_axis=3, tiled=True)
    state_in = returned[0].reshape(batch_count, local_heads, head_width, state_width)
    gated_list = []
    square_list = []
    for block_index in range(blocks):
        lower = block_index * GROUP
        upper = lower + GROUP
        total_state = (
            local_list[block_index] + before_list[block_index][:, :, None, None] * state_in
        )
        carried = jnp.einsum(
            "bhpn,btn->bthp", total_state, c_list[block_index], precision=lax.Precision.HIGHEST
        )
        inside = jnp.exp(cumulative[:, lower:upper])
        value_block = (
            value_conv[:, lower:upper]
            .reshape(batch_count, GROUP, local_heads, head_width)
            .astype(jnp.float32)
        )
        mixture = (
            within_list[block_index]
            + inside[:, :, :, None] * carried
            + skip_gain[None, None, :, None] * value_block
        )
        gated = mixture.reshape(batch_count, GROUP, local_inner) * jax.nn.silu(
            gate_part[:, lower:upper].astype(jnp.float32)
        )
        gated_list.append(gated)
        square_list.append(jnp.sum(gated * gated, axis=-1))
    squares = of_everyone(jnp.concatenate(square_list, axis=-1), "head")
    inverse = lax.rsqrt(squares / INNER + EPS)
    outputs = []
    for block_index in range(blocks):
        lower = block_index * GROUP
        upper = lower + GROUP
        outputs.append(
            (gated_list[block_index] * inverse[:, lower:upper, None] * norm_gain).astype(
                jnp.bfloat16
            )
        )
    return jnp.concatenate(outputs, axis=1)


def solution(mesh):
    finer = Mesh(
        mesh.devices.reshape(4, 4, 2, mesh.shape["head"]), ("seq_0", "seq_1", "seq_2", "head")
    )
    return jax.shard_map(
        local,
        mesh=finer,
        in_specs=(
            P(None, SEQ, None),
            P(None, "head"),
            P(None, "head"),
            P(),
            P(None, "head"),
            P(None, "head"),
            P("head"),
            P(),
            P(),
            P("head"),
            P("head"),
            P("head"),
            P("head"),
        ),
        out_specs=P(None, SEQ, "head"),
        check_vma=False,
    )
```

profile of v0, /device:TPU:1, one launch (start us, length us, event | category | flops | bytes accessed | tf_op | source)
XLA Modules:
  0.0 159.5 jit_solution(9992299238188705038)
XLA Ops:
  0.0 10.9 %fusion.22 = bf16[2,512,1280]{2,1,0:T(8,128)(2,1)S(1)} fusion(bf16[2,512,2560]{2,1,0:T(8,128)(2,1)} %param.13, bf16[2560,1280]{1,0:T(8,128)(2,1)} %param.15), kind=kOutput, calls=%fused_computation.31 | convolution fusion | flops 6712197120 | bytes 14417920 | tf_op jit(solution)/shard_map/btd,dc->btc/dot_general | solution.py:99
  11.0 1.5 fusion.51
  12.6 5.1 %collective-permute-start = (bf16[2,3,1536]{2,1,0:T(4,128)(2,1)S(1)}, bf16[2,3,1536]{2,1,0:T(4,128)(2,1)S(1)}, u32[]{:S(2)}, u32[]{:S(2)}) collective-permute-start(bf16[2,3,1536]{2,1,0:T(4,128)(2,1)S(1)} %pad_maximum_fusion.1), channel_id=1, source_target_pairs={{0,4},{4,8},{8,12},{12,16},{16,20},{20,24},{24,28},{28,32},{32,36}... | collective-permute-start | bytes 55304 | tf_op jit(solution)/shard_map/ppermute | solution.py:18
  17.8 1.5 negate_multiply_fusion
  19.5 2.3 %reduce-window.6 = f32[2,2,20,2,128]{4,2,3,1,0:T(8,128)S(1)} reduce-window(f32[2,2,20,2,128]{4,2,3,1,0:T(8,128)S(1)} %copy.128, f32[]{:T(128)} %constant.21.clone.1), window={size=1x1x1x1x128 pad=0_0x0_0x0_0x0_0x127_0}, to_apply=%region_0.1 | reduce-window | flops 2600960 | bytes 163844 | tf_op jit(solution)/shard_map/reduce-window
  22.7 0.6 bitcast_exponential_fusion
  23.3 0.7 exponential_multiply_fusion.1
  24.2 0.7 multiply_convert_fusion.11
  24.9 0.7 slice_convert_fusion.1
  25.7 0.4 copy-done.8
  26.0 0.5 maximum_convert_fusion
  26.7 3.4 %multiply_convert_fusion.2 = bf16[2,512,1280]{2,1,0:T(8,128)(2,1)S(1)} fusion(f32[2,515,1280]{2,1,0:T(8,128)S(1)} %maximum_convert_fusion, f32[1280]{0:T(1024)S(1)} %get-tuple-element.9, f32[1280]{0:T(1024)S(1)} %get-tuple-element.10, f32[1280]{0:T(1024)S(1)} %get-tuple-element.8, f32[1280]{0:T(1024)S(1)} %get-tuple-element.7, f32[1280]{0:T(1024)S(1)} %copy-done.19), kind=kLoop, calls=%fused_computation.28 | loop fusion | flops 17039360 | bytes 23618560 | tf_op jit(solution)/shard_map/convert_element_type | solution.py:71
  30.3 1.5 copy.125
  31.8 0.6 copy.134
  32.5 4.3 %fusion.45 = f32[2,20,64,128]{3,2,1,0:T(8,128)S(1)} fusion(bf16[2,256,20,64]{1,3,2,0:T(8,128)(2,1)} %bitcast.108, f32[2,256,128]{2,1,0:T(8,128)} %get-tuple-element.15, f32[2,256,20]{1,2,0:T(8,128)} %get-tuple-element.17, f32[2,20]{1,0:T(2,128)} %get-tuple-element.34), kind=kOutput, calls=%fused_computation.62 | convolution fusion | flops 170721280 | bytes 2924704 | tf_op jit(solution)/shard_map/bshp,bshn->bhpn/dot_general | solution.py:151
  36.8 1.0 copy-done.5
  37.9 3.2 %fusion.44 = f32[2,20,64,128]{3,2,1,0:T(8,128)} fusion(bf16[2,256,20,64]{1,3,2,0:T(8,128)(2,1)S(1)} %bitcast.104, f32[2,256,128]{2,1,0:T(8,128)S(1)} %get-tuple-element.16, f32[2,256,20]{1,2,0:T(8,128)S(1)} %get-tuple-element.18, f32[2,20,64,128]{3,2,1,0:T(8,128)S(1)} %fusion.45, f32[2,20]{1,0:T(2,128)S(1)} %copy-done.18), kind=kOutput, calls=%fused_computation.61 | convolution fusion | flops 171048960 | bytes 4235424 | tf_op jit(solution)/shard_map/bshp,bshn->bhpn/dot_general | solution.py:151
  41.1 1.6 %reshape_broadcast_in_dim_reshape.3 = f32[1,2,20,32,256]{4,3,2,1,0:T(8,128)S(1)} reshape(f32[2,20,64,128]{3,2,1,0:T(8,128)} %fusion.44) | data formatting | bytes 2621440 | tf_op jit(solution)/shard_map/reshape;broadcast_in_dim;reshape | solution.py:23
  42.8 1.0 copy.136
  43.8 0.8 copy.137
  44.6 4.4 %all_to_all.35 = f32[16,2,1,2,20,256]{5,0,4,3,2,1:T(8,128)S(1)} all-to-all(f32[16,2,1,2,20,256]{5,0,4,3,2,1:T(8,128)S(1)} %copy.137), channel_id=1, replica_groups=mesh['seq_0'=4,'seq_1'=4,'seq_2'=2,'head'=4] {'seq_2'}, dimensions={1} | all-to-all | bytes 2621440 | tf_op jit(solution)/shard_map/all_to_all | solution.py:36
  49.0 0.6 broadcast_in_dim.58
  49.6 7.8 %all-to-all-start.2 = ((f32[32,1,2,20]{3,2,1,0:T(2,128)}), f32[32,1,2,20]{3,2,1,0:T(2,128)S(1)}, u32[]{:S(2)}, u32[]{:S(2)}) async-start(f32[32,1,2,20]{3,2,1,0:T(2,128)} %broadcast_in_dim.58), calls=%async_computation.2 | async-start | bytes 65536 | tf_op jit(solution)/shard_map/all_to_all | solution.py:48
  57.4 2.1 %copy.138 = f32[16,2,1,2,20,256]{5,1,4,3,2,0:T(2,128)} copy(f32[16,2,1,2,20,256]{5,0,4,3,2,1:T(8,128)S(1)} %all_to_all.35) | data formatting | bytes 2621440 | tf_op jit(solution)/shard_map/all_to_all | solution.py:36
  59.5 5.2 %all-to-all-done.2 = f32[32,1,2,20]{3,2,1,0:T(2,128)S(1)} async-done(((f32[32,1,2,20]{3,2,1,0:T(2,128)}), f32[32,1,2,20]{3,2,1,0:T(2,128)S(1)}, u32[]{:S(2)}, u32[]{:S(2)}) %all-to-all-start.2) | async-done | bytes 5152 | tf_op jit(solution)/shard_map/all_to_all | solution.py:48
  64.7 3.9 %all-to-all-start.1 = ((f32[16,2,1,2,20,256]{5,1,4,3,2,0:T(2,128)}), f32[16,2,1,2,20,256]{5,1,4,3,2,0:T(2,128)S(1)}, u32[]{:S(2)}, u32[]{:S(2)}) async-start(f32[16,2,1,2,20,256]{5,1,4,3,2,0:T(2,128)} %copy.138), calls=%async_computation.1 | async-start | bytes 2621440 | tf_op jit(solution)/shard_map/all_to_all | solution.py:36
  68.9 19.5 %all-to-all-done.1 = f32[16,2,1,2,20,256]{5,1,4,3,2,0:T(2,128)S(1)} async-done(((f32[16,2,1,2,20,256]{5,1,4,3,2,0:T(2,128)}), f32[16,2,1,2,20,256]{5,1,4,3,2,0:T(2,128)S(1)}, u32[]{:S(2)}, u32[]{:S(2)}) %all-to-all-start.1) | async-done | bytes 1310752 | tf_op jit(solution)/shard_map/all_to_all | solution.py:36
  88.4 0.7 copy.139
  89.1 0.9 reshape_reshape.3
  90.0 1.4 convolution_bitcast_fusion
  91.5 2.1 %copy.143 = f32[32,2,20,256]{3,1,2,0:T(2,128)} copy(f32[32,2,20,256]{3,0,2,1:T(8,128)S(1)} %convolution_bitcast_fusion) | data formatting | bytes 2621440 | tf_op jit(solution)/shard_map/jibh,ibhs->jbhs/transpose | solution.py:170
  93.5 5.5 %all-to-all-start.3 = ((f32[32,2,20,256]{3,1,2,0:T(2,128)}), f32[32,2,20,256]{3,1,2,0:T(2,128)S(1)}, u32[]{:S(2)}, u32[]{:S(2)}) async-start(f32[32,2,20,256]{3,1,2,0:T(2,128)} %copy.143), calls=%async_computation.3 | async-start | bytes 2621440 | tf_op jit(solution)/shard_map/all_to_all | solution.py:171
  99.0 11.9 %fusion.25 = bf16[2,512,1280]{2,1,0:T(8,128)(2,1)} fusion(bf16[2,512,2560]{2,1,0:T(8,128)(2,1)} %param.13, bf16[2560,1280]{1,0:T(8,128)(2,1)} %param.14), kind=kOutput, calls=%fused_computation.32 | convolution fusion | flops 6712197120 | bytes 14417920 | tf_op jit(solution)/shard_map/btd,dc->btc/dot_general | solution.py:96
  110.9 1.1 fusion.72
  112.0 1.0 fusion.75
  113.0 5.9 %all-to-all-done.3 = f32[32,2,20,256]{3,1,2,0:T(2,128)S(1)} async-done(((f32[32,2,20,256]{3,1,2,0:T(2,128)}), f32[32,2,20,256]{3,1,2,0:T(2,128)S(1)}, u32[]{:S(2)}, u32[]{:S(2)}) %all-to-all-start.3) | async-done | bytes 1310752 | tf_op jit(solution)/shard_map/all_to_all | solution.py:171
  118.9 0.4 copy.144
  119.4 2.7 %fusion.68 = f32[2,256,20,64]{1,3,2,0:T(8,128)} fusion(f32[2,20,64,128]{3,2,1,0:T(8,128)S(1)} %reshape_squeeze.3, bf16[2,512,256]{2,1,0:T(8,128)(2,1)S(1)} %multiply_convert_fusion.11), kind=kOutput, calls=%fused_computation.93 | convolution fusion | flops 1006632960 | bytes 4063232 | tf_op jit(solution)/shard_map/bhpn,btn->bthp/dot_general | solution.py:181
  122.2 1.2 fusion.48
  123.6 4.6 %fusion.38 = f32[2,256,20,64]{1,3,2,0:T(8,128)} fusion(bf16[2,256,20,64]{1,3,2,0:T(8,128)(2,1)S(1)} %bitcast.105, f32[2,256,20,64]{1,3,2,0:T(8,128)S(1)} %fusion.48, f32[2,256,20]{1,2,0:T(8,128)S(1)} %copy-done.15, f32[2,256,20]{1,2,0:T(8,128)S(1)} %copy-done.16, f32[2,256,256]{2,1,0:T(8,128)S(1)} %copy-done.11, pred[256,256]{1,0:T(8,128)(4,1)S(1)} %iota_compare_fusion, ...), kind=kOutput, calls=%fused_computation.50 | convolution fusion | flops 354549760 | bytes 7266384 | tf_op jit(solution)/shard_map/btsh,bshp->bthp/dot_general | solution.py:145
  128.2 3.4 %copy.146 = f32[2,256,1280]{2,1,0:T(8,128)} copy(f32[2,256,1280]{1,2,0:T(8,128)} %bitcast.107) | data formatting | bytes 5242880 | tf_op jit(solution)/shard_map/reshape | solution.py:195
  131.6 6.1 %fusion.39 = f32[2,256,20,64]{1,3,2,0:T(8,128)} fusion(bf16[2,256,20,64]{1,3,2,0:T(8,128)(2,1)S(1)} %bitcast.109, f32[2,256,20,64]{1,3,2,0:T(8,128)} %fusion.68, f32[2,256,20]{1,2,0:T(8,128)S(1)} %get-tuple-element.21, f32[2,256,20]{1,2,0:T(8,128)S(1)} %copy-done.13, f32[2,256,256]{2,1,0:T(8,128)S(1)} %copy-done.10, ...), kind=kOutput, calls=%fused_computation.52 | convolution fusion | flops 354549760 | bytes 7266384 | tf_op jit(solution)/shard_map/btsh,bshp->bthp/dot_general | solution.py:145
  137.7 3.2 %copy.145 = f32[2,256,1280]{2,1,0:T(8,128)} copy(f32[2,256,1280]{1,2,0:T(8,128)} %bitcast.106) | data formatting | bytes 5242880 | tf_op jit(solution)/shard_map/reshape | solution.py:195
  140.9 4.2 %multiply_reduce_fusion.1 = (f32[2,256]{1,0:T(2,128)S(1)}, f32[2,256]{1,0:T(2,128)S(1)}) fusion(f32[2,256,1280]{2,1,0:T(8,128)} %copy.145, bf16[2,512,1280]{2,1,0:T(8,128)(2,1)} %fusion.25, f32[2,256,1280]{2,1,0:T(8,128)} %copy.146), kind=kLoop, calls=%fused_computation.56 | loop fusion | flops 10484736 | bytes 7868416 | tf_op jit(solution)/shard_map/reduce_sum | solution.py:199
  145.1 0.6 broadcast_in_dim.103
  145.7 4.2 %all-to-all-start.4 = ((f32[4,2,512]{2,1,0:T(2,128)}), f32[4,2,512]{2,1,0:T(2,128)S(1)}, u32[]{:S(2)}, u32[]{:S(2)}) async-start(f32[4,2,512]{2,1,0:T(2,128)} %broadcast_in_dim.103), calls=%async_computation.4 | async-start | bytes 32768 | tf_op jit(solution)/shard_map/all_to_all | solution.py:48
  149.9 4.2 %all-to-all-done.4 = f32[4,2,512]{2,1,0:T(2,128)S(1)} async-done(((f32[4,2,512]{2,1,0:T(2,128)}), f32[4,2,512]{2,1,0:T(2,128)S(1)}, u32[]{:S(2)}, u32[]{:S(2)}) %all-to-all-start.4) | async-done | bytes 16416 | tf_op jit(solution)/shard_map/all_to_all | solution.py:48
  154.2 5.3 %multiply_convert_fusion.6 = (bf16[2,512,1280]{2,1,0:T(8,128)(2,1)}, bf16[2,512,1280]{2,1,0:T(8,128)(2,1)}) fusion(f32[1280]{0:T(1024)S(1)} %copy-done.20, f32[2,256]{1,0:T(2,128)S(1)} %get-tuple-element.27, f32[2,256,1280]{2,1,0:T(8,128)} %copy.145, bf16[2,512,1280]{2,1,0:T(8,128)(2,1)} %fusion.25, ...), kind=kLoop, output_to_operand_aliasing={{0}: (6, {}), {1}: (6, {})}, calls=%fused_computation.54 | loop fusion | flops 11796480 | bytes 10494976 | tf_op jit(solution)/shard_map/convert_element_type | solution.py:207
  (89 shorter events, 2.2 us)
Async XLA Ops:
  0.0 11.0 %copy-start = (bf16[2560,256]{1,0:T(8,128)(2,1)S(1)}, bf16[2560,256]{1,0:T(8,128)(2,1)}, u32[]{:S(2)}) copy-start(bf16[2560,256]{1,0:T(8,128)(2,1)} %param.16) | copy-start | bytes 3932164
  0.0 11.0 %copy-start.2 = (bf16[2,512,2560]{2,1,0:T(8,128)(2,1)S(1)}, bf16[2,512,2560]{2,1,0:T(8,128)(2,1)}, u32[]{:S(2)}) copy-start(bf16[2,512,2560]{2,1,0:T(8,128)(2,1)} %param.13) | copy-start | bytes 15728644
  10.9 1.6 %copy-start.7 = (bf16[2,512,1280]{2,1,0:T(8,128)(2,1)}, bf16[2,512,1280]{2,1,0:T(8,128)(2,1)S(1)}, u32[]{:S(2)}) copy-start(bf16[2,512,1280]{2,1,0:T(8,128)(2,1)S(1)} %fusion.22) | copy-start | bytes 7864324
  11.0 6.7 %copy-start.12 = (bf16[2560,20]{0,1:T(8,128)(2,1)S(1)}, bf16[2560,20]{0,1:T(8,128)(2,1)}, u32[]{:S(2)}) copy-start(bf16[2560,20]{0,1:T(8,128)(2,1)} %param.17) | copy-start | bytes 307204
  11.0 6.7 %copy-start.24 = (f32[20]{0:T(128)S(1)}, f32[20]{0:T(128)}, u32[]{:S(2)}) copy-start(f32[20]{0:T(128)} %param.23) | copy-start | bytes 244
  11.0 6.7 %copy-start.25 = (f32[20]{0:T(128)S(1)}, f32[20]{0:T(128)}, u32[]{:S(2)}) copy-start(f32[20]{0:T(128)} %param.22) | copy-start | bytes 244
  12.6 10.0 %copy-start.22 = (f32[4,256]{1,0:T(4,128)S(1)}, f32[4,256]{1,0:T(4,128)}, u32[]{:S(2)}) copy-start(f32[4,256]{1,0:T(4,128)} %param.20) | copy-start | bytes 12292
  12.6 11.4 %copy-start.17 = (f32[4,1280]{1,0:T(4,128)S(1)}, f32[4,1280]{1,0:T(4,128)}, u32[]{:S(2)}) copy-start(f32[4,1280]{1,0:T(4,128)} %param.18) | copy-start | bytes 61444
  12.6 11.4 %collective-permute-start = (bf16[2,3,1536]{2,1,0:T(4,128)(2,1)S(1)}, bf16[2,3,1536]{2,1,0:T(4,128)(2,1)S(1)}, u32[]{:S(2)}, u32[]{:S(2)}) collective-permute-start(bf16[2,3,1536]{2,1,0:T(4,128)(2,1)S(1)} %pad_maximum_fusion.1), channel_id=1, source_target_pairs={{0,4},{4,8},{8,12},{12,16},{16,20},{20,24},{24,28},{28,32},{32,36}... | collective-permute-start | bytes 55304 | tf_op jit(solution)/shard_map/ppermute | solution.py:18
  19.3 4.9 %copy-start.26 = (f32[256]{0:T(256)S(1)}, f32[256]{0:T(256)}, u32[]{:S(2)}) copy-start(f32[256]{0:T(256)} %param.21) | copy-start | bytes 3076
  24.2 1.8 %copy-start.8 = (bf16[2,512,1280]{2,1,0:T(8,128)(2,1)S(1)}, bf16[2,512,1280]{2,1,0:T(8,128)(2,1)}, u32[]{:S(2)}) copy-start(bf16[2,512,1280]{2,1,0:T(8,128)(2,1)} %copy-done.7) | copy-start | bytes 7864324
  26.0 0.7 copy-start.19
  32.4 8.7 %copy-start.3 = (bf16[2,256,1280]{1,2,0:T(8,128)(2,1)}, bf16[2,256,1280]{1,2,0:T(8,128)(2,1)S(1)}, u32[]{:S(2)}) copy-start(bf16[2,256,1280]{1,2,0:T(8,128)(2,1)S(1)} %copy.134) | copy-start | bytes 3932164
  32.5 5.4 %copy-start.18 = (f32[2,20]{1,0:T(2,128)S(1)}, f32[2,20]{1,0:T(2,128)}, u32[]{:S(2)}) copy-start(f32[2,20]{1,0:T(2,128)} %get-tuple-element.36) | copy-start | bytes 484
  36.8 1.1 copy-start.5
  43.8 5.2 %copy-start.23 = (f32[2,20]{1,0:T(2,128)S(1)}, f32[2,20]{1,0:T(2,128)}, u32[]{:S(2)}) copy-start(f32[2,20]{1,0:T(2,128)} %get-tuple-element.35) | copy-start | bytes 484
  49.6 15.1 %all-to-all-start.2 = ((f32[32,1,2,20]{3,2,1,0:T(2,128)}), f32[32,1,2,20]{3,2,1,0:T(2,128)S(1)}, u32[]{:S(2)}, u32[]{:S(2)}) async-start(f32[32,1,2,20]{3,2,1,0:T(2,128)} %broadcast_in_dim.58), calls=%async_computation.2 | async-start | bytes 65536 | tf_op jit(solution)/shard_map/all_to_all | solution.py:48
  64.7 23.7 %all-to-all-start.1 = ((f32[16,2,1,2,20,256]{5,1,4,3,2,0:T(2,128)}), f32[16,2,1,2,20,256]{5,1,4,3,2,0:T(2,128)S(1)}, u32[]{:S(2)}, u32[]{:S(2)}) async-start(f32[16,2,1,2,20,256]{5,1,4,3,2,0:T(2,128)} %copy.138), calls=%async_computation.1 | async-start | bytes 2621440 | tf_op jit(solution)/shard_map/all_to_all | solution.py:36
  93.5 25.4 %all-to-all-start.3 = ((f32[32,2,20,256]{3,1,2,0:T(2,128)}), f32[32,2,20,256]{3,1,2,0:T(2,128)S(1)}, u32[]{:S(2)}, u32[]{:S(2)}) async-start(f32[32,2,20,256]{3,1,2,0:T(2,128)} %copy.143), calls=%async_computation.3 | async-start | bytes 2621440 | tf_op jit(solution)/shard_map/all_to_all | solution.py:171
  119.4 2.7 %copy-start.6 = (f32[2,20,64,128]{3,2,1,0:T(8,128)S(1)}, f32[2,20,64,128]{3,2,1,0:T(8,128)}, u32[]{:S(2)}) copy-start(f32[2,20,64,128]{3,2,1,0:T(8,128)} %copy-done.5) | copy-start | bytes 3932164
  119.4 2.7 %copy-start.21 = (f32[2,20]{1,0:T(2,128)S(1)}, f32[2,20]{1,0:T(2,128)}, u32[]{:S(2)}) copy-start(f32[2,20]{1,0:T(2,128)} %get-tuple-element.33) | copy-start | bytes 484
  122.1 1.3 copy-start.4
  122.1 1.4 copy-start.11
  122.1 1.4 copy-start.14
  122.1 1.4 copy-start.15
  122.1 1.4 copy-start.16
  122.1 1.4 copy-start.27
  128.2 3.4 %copy-start.9 = (bf16[2,256,1280]{1,2,0:T(8,128)(2,1)S(1)}, bf16[2,256,1280]{1,2,0:T(8,128)(2,1)}, u32[]{:S(2)}) copy-start(bf16[2,256,1280]{1,2,0:T(8,128)(2,1)} %copy.125) | copy-start | bytes 3932164
  128.2 3.4 %copy-start.10 = (f32[2,256,256]{2,1,0:T(8,128)S(1)}, f32[2,256,256]{2,1,0:T(8,128)}, u32[]{:S(2)}) copy-start(f32[2,256,256]{2,1,0:T(8,128)} %fusion.75) | copy-start | bytes 1572868
  128.2 3.4 %copy-start.13 = (f32[2,256,20]{1,2,0:T(8,128)S(1)}, f32[2,256,20]{1,2,0:T(8,128)}, u32[]{:S(2)}) copy-start(f32[2,256,20]{1,2,0:T(8,128)} %get-tuple-element.24) | copy-start | bytes 122884
  140.9 13.2 %copy-start.20 = (f32[1280]{0:T(1024)S(1)}, f32[1280]{0:T(1024)}, u32[]{:S(2)}) copy-start(f32[1280]{0:T(1024)} %param.25) | copy-start | bytes 15364
  145.7 8.4 %all-to-all-start.4 = ((f32[4,2,512]{2,1,0:T(2,128)}), f32[4,2,512]{2,1,0:T(2,128)S(1)}, u32[]{:S(2)}, u32[]{:S(2)}) async-start(f32[4,2,512]{2,1,0:T(2,128)} %broadcast_in_dim.103), calls=%async_computation.4 | async-start | bytes 32768 | tf_op jit(solution)/shard_map/all_to_all | solution.py:48
  154.2 5.3 %copy-start.1 = (bf16[2560,256]{1,0:T(8,128)(2,1)S(1)}, bf16[2560,256]{1,0:T(8,128)(2,1)}, u32[]{:S(2)}) copy-start(bf16[2560,256]{1,0:T(8,128)(2,1)} %param.16) | copy-start | bytes 3932164
where the time goes:
time: 161 us; the launch traced here: 160 us
  matrix products  51.6 us (32%)
  waiting for transfers between devices  34.8 us (22%)
  starting transfers between devices  26.5 us (16%)
  local copies, waits for them, and re-layouts  22.8 us (14%)
  other arithmetic  18.8 us (12%)
  blocking collectives  4.42 us (3%)
    all_to_all x1, waiting for transfers between devices, turned_blocks(): out = lax.all_to_all(out, axes[k], k, k, tiled=True)  19.5 us
    all_to_all x2, starting transfers between devices, copy_for_each(): lax.all_to_all(jnp.broadcast_to(array[None], (count, *array.shape)), axis...  12 us
    dot_general x1, matrix products, local(): jnp.einsum('btd,dc->btc', tokens, gate_weight, preferred_element_type=jnp...  11.9 us
    dot_general x1, matrix products, local(): jnp.einsum('btd,dc->btc', tokens, value_weight, preferred_element_type=jn...  10.9 us
    dot_general x2, matrix products, local(): jnp.einsum('btsh,bshp->bthp', mixing, value_block, preferred_element_type...  10.8 us
    all_to_all x2, waiting for transfers between devices, copy_for_each(): lax.all_to_all(jnp.broadcast_to(array[None], (count, *array.shape)), axis...  9.42 us
    dot_general x2, matrix products, local(): jnp.einsum('bshp,bshn->bhpn', value_block, weighted, preferred_element_ty...  7.57 us
    reshape x2, local copies, waits for them, and re-layouts, local(): mixture.reshape(batch_count, GROUP, local_inner)  6.57 us
  transfers between devices with their start and end apart: 5, of which 4 were waited for; matrix products, arithmetic and copies ran while one was open for 14% of the time, Pallas kernels for 0%

commit v1 on v0

v1 whole, which is shorter than its diff:
```python
import functools

import jax
import jax.numpy as jnp
from jax import lax
from jax.experimental import pallas as pl
from jax.experimental.pallas import tpu as pltpu
from jax.sharding import PartitionSpec as P

MESH = pl.DeviceIdType.MESH
F32 = jnp.float32
BF16 = jnp.bfloat16

EPS = 1e-05
LOG2E = 1.4426950408889634
B = 2
T = 512
D = 2560
C = 1280
H = 20
N = 128
L = 128
K = T // L
GC = 256
G = C // GC
HALO = 16
R = T + HALO
TAPS = 4
PEERS = 32
HEADS_AXIS = 4
INNER = 5120


def dot(a, b):
    return jnp.dot(a, b, preferred_element_type=F32)


def split3(x):
    hi = x.astype(BF16).astype(F32)
    rest = x - hi
    mid = rest.astype(BF16).astype(F32)
    return hi, mid, rest - mid


def packed(x):
    lane = lax.broadcasted_iota(jnp.int32, x.shape, 1)
    hi, mid, low = split3(jnp.where(lane < H, x, 0.0))
    return (hi + pltpu.roll(mid, 32, 1) + pltpu.roll(low, 64, 1)).astype(BF16)


def silu(x):
    half = 0.5 * x
    return half * jnp.tanh(half) + half


def spread_matrix(shape, first_head, width):
    row = lax.broadcasted_iota(jnp.int32, shape, 0)
    col = lax.broadcasted_iota(jnp.int32, shape, 1)
    hit = (row & 31) == (first_head + col // width)
    return jnp.where(hit & (row < 96), 1.0, 0.0).astype(BF16)


def body(
    tok, gate_w, value_w, state_w, step_w,
    value_k, value_o, state_k, state_o, step_o, decay, skip, gain,
    out,
    x, wv, wg, ws, wd, cv, vbuf, gbuf, mixbuf, brow_t, crow, sc, a3, a2w, a2g, cs_t,
    e512, e256, eh, rows_t, rows_b, rows_s, pad, local, sendbuf, recvbuf, retbuf, retrecv,
    logsend, logrecv, fac, sq, ssend, srecv, obuf,
    xsem, vsem, gsem, msem, osem, hsem, ssem, rsem, tsem, usem, lsem, qsem,
):
    me = lax.axis_index("seq")
    hd = lax.axis_index("head")

    x_copies = [
        pltpu.make_async_copy(tok.at[b], x.at[b, pl.ds(HALO, T)], xsem.at[b]) for b in range(B)
    ]
    s_copy = pltpu.make_async_copy(state_w, ws, msem.at[0])
    d_copy = pltpu.make_async_copy(step_w, wd, msem.at[1])

    def v_copy(g):
        return pltpu.make_async_copy(
            value_w.at[:, pl.ds(pl.multiple_of(g * GC, GC), GC)], wv.at[g], vsem.at[g]
        )

    def g_copy(g):
        return pltpu.make_async_copy(
            gate_w.at[:, pl.ds(pl.multiple_of(g * GC, GC), GC)], wg.at[g], gsem.at[g]
        )

    d_copy.start()
    for c in x_copies:
        c.start()
    s_copy.start()
    for g in range(G):
        v_copy(g).start()
    for g in range(G):
        g_copy(g).start()

    barrier = pltpu.get_barrier_semaphore()

    def greet(d, _):
        pl.semaphore_signal(
            barrier, inc=1, device_id={"seq": lax.rem(me + d, PEERS)}, device_id_type=MESH
        )
        return 0

    lax.fori_loop(1, PEERS, greet, 0)
    for d in range(1, HEADS_AXIS):
        pl.semaphore_signal(
            barrier, inc=1, device_id={"head": lax.rem(hd + d, HEADS_AXIS)}, device_id_type=MESH
        )

    for g in range(G):
        e512[g] = spread_matrix((128, 512), 4 * g, 128)
        e256[g] = spread_matrix((128, 256), 4 * g, 64)
        for h in range(2):
            eh[h, g] = spread_matrix((128, 128), 2 * (2 * g + h), 64)
    pad[...] = jnp.zeros_like(pad)
    pad[0:1, 0:H] = step_o[...]
    pad[8:9, 0:H] = decay[...]
    pad[16:17, 0:H] = skip[...]
    sq[...] = jnp.zeros_like(sq)

    pl.semaphore_wait(barrier, PEERS - 1 + HEADS_AXIS - 1)

    def halo_copy(dest):
        return pltpu.make_async_remote_copy(
            src_ref=tok.at[:, pl.ds(T - HALO, HALO)],
            dst_ref=x.at[:, pl.ds(0, HALO)],
            send_sem=hsem.at[0],
            recv_sem=hsem.at[1],
            device_id={"seq": dest},
            device_id_type=MESH,
        )

    @pl.when(me < PEERS - 1)
    def _():
        halo_copy(me + 1).start()

    @pl.when(me == 0)
    def _():
        x[:, 0:HALO, :] = jnp.zeros((B, HALO, D), BF16)

    d_copy.wait()
    for c in x_copies:
        c.wait()
    tri = lax.broadcasted_iota(jnp.int32, (L, L), 0) >= lax.broadcasted_iota(jnp.int32, (L, L), 1)
    tri16 = jnp.where(tri, 1.0, 0.0).astype(BF16)
    tri3 = jnp.concatenate([tri16, tri16, tri16], axis=1)
    logsend[...] = jnp.zeros_like(logsend)
    for b in range(B):
        a3f = dot(x[b, HALO:R], wd[...])
        sq[b, :, 0:H] = a3f
        z = sq[b] + pad[0:1]
        step = jnp.maximum(z, 0.0) + jnp.log1p(jnp.exp(-jnp.abs(z)))
        decayed = step * (pad[8:9] * (-LOG2E))
        log_step = jnp.log(step) * LOG2E
        before = jnp.zeros((1, 128), F32)
        for k in range(K):
            part = decayed[k * L : (k + 1) * L]
            hi, mid, low = split3(part)
            stacked = jnp.concatenate([hi, mid, low], axis=0).astype(BF16)
            cum = dot(tri3, stacked)
            last = cum[L - 1 : L]
            source = cum - log_step[k * L : (k + 1) * L]
            a3[b, k] = packed(cum)
            a2w[b, k] = packed(jnp.exp2(last - source))
            a2g[b, k] = packed(jnp.exp2(cum))
            cs_t[b, k] = jnp.transpose(source)[0:32]
            pad[24 + b * K + k : 25 + b * K + k] = jnp.exp2(last)
            pad[32 + b * K + k : 33 + b * K + k] = jnp.exp2(before)
            before = before + last
        logsend[b : b + 1] = before
    sq[...] = jnp.zeros_like(sq)

    def log_copy(dest):
        return pltpu.make_async_remote_copy(
            src_ref=logsend,
            dst_ref=logrecv.at[me],
            send_sem=lsem.at[0],
            recv_sem=lsem.at[1],
            device_id={"seq": dest},
            device_id_type=MESH,
        )

    def send_log(d, _):
        log_copy(lax.rem(me + d, PEERS)).start()
        return 0

    lax.fori_loop(1, PEERS, send_log, 0)
    logrecv[me] = logsend[...]

    rt = packed(pad[24:32])
    rb = packed(pad[32:40])
    rs = packed(pad[16:24])
    for g in range(G):
        rows_t[g] = dot(rt, e256[g])
        rows_b[g] = dot(rb, e256[g])
        rows_s[g] = dot(rs, e256[g])

    s_copy.wait()

    @pl.when(me > 0)
    def _():
        halo_copy(me).wait_recv()

    def convolve(b, raw, taps, offset, j):
        cv[b, j] = raw.astype(BF16).astype(F32)
        total = offset
        for tap in range(TAPS):
            total = total + taps[tap : tap + 1] * cv[b, j, pl.ds(HALO - TAPS + 1 + tap, T), :]
        return silu(total).astype(BF16)

    for b in range(B):
        raw = dot(x[b], ws[...])
        bmap = convolve(b, raw[:, 0:N], state_k[:, 0:N], state_o[:, 0:N], 0)
        cmap = convolve(b, raw[:, N : 2 * N], state_k[:, N : 2 * N], state_o[:, N : 2 * N], 1)
        for k in range(K):
            bk = bmap[k * L : (k + 1) * L]
            ck = cmap[k * L : (k + 1) * L]
            crow[b, k] = ck
            bt = jnp.transpose(bk.astype(F32)).astype(BF16)
            brow_t[b, k] = bt
            sc[b, k] = jnp.where(tri, dot(ck, bt), 0.0)

    def share_copy(g, dest):
        return pltpu.make_async_remote_copy(
            src_ref=sendbuf.at[g, dest],
            dst_ref=recvbuf.at[g, me],
            send_sem=ssem.at[g],
            recv_sem=rsem.at[g],
            device_id={"seq": dest},
            device_id_type=MESH,
        )

    def back_copy(g, dest):
        return pltpu.make_async_remote_copy(
            src_ref=retbuf.at[g, dest],
            dst_ref=retrecv.at[g, me],
            send_sem=tsem.at[g],
            recv_sem=usem.at[g],
            device_id={"seq": dest},
            device_id_type=MESH,
        )

    def value_group(g, _):
        v_copy(g).wait()
        base = pl.multiple_of(g * GC, GC)
        for b in range(B):
            raw = dot(x[b], wv[g])
            for j in range(2):
                at = pl.ds(pl.multiple_of(base + j * 128, 128), 128)
                vbuf[g, b, :, j * 128 : (j + 1) * 128] = convolve(
                    b, raw[:, j * 128 : (j + 1) * 128], value_k[:, at], value_o[:, at], j
                )
            state = None
            for k in range(K):
                scale = dot(a2w[b, k], e256[g])
                vk = vbuf[g, b, k * L : (k + 1) * L].astype(F32)
                made = dot(brow_t[b, k], (vk * scale).astype(BF16))
                if state is None:
                    state = made
                else:
                    local[g, b, k - 1] = state
                    state = state * rows_t[g, b * K + k : b * K + k + 1] + made
            state = state.astype(BF16)
            for h in range(2):
                first = (b * 2 + h) * 8
                sendbuf[g, first : first + 8] = state[:, h * 128 : (h + 1) * 128].reshape(8, 16, 128)

        def send(d, _):
            share_copy(g, lax.rem(me + d, PEERS)).start()
            return 0

        lax.fori_loop(1, PEERS, send, 0)
        recvbuf[g, me] = sendbuf[g, me]
        return 0

    lax.fori_loop(0, G, value_group, 0)

    def all_logs():
        return pltpu.make_async_remote_copy(
            src_ref=logrecv.at[pl.ds(0, PEERS - 1)],
            dst_ref=logrecv.at[pl.ds(0, PEERS - 1)],
            send_sem=lsem.at[0],
            recv_sem=lsem.at[1],
            device_id={"seq": me},
            device_id_type=MESH,
        )

    all_logs().wait_recv()
    my_batch = me // 16
    my_half = lax.rem(me // 8, 2)
    logs = logrecv[:, pl.ds(my_batch, 1), :].reshape(PEERS, 128)
    through = packed(jnp.exp2(logs))
    for g in range(G):
        fac[g] = dot(through, eh[my_half, g])

    first_half = lax.broadcasted_iota(jnp.int32, (L, 128), 1) < 64

    def bulk(buf, g, send, recv):
        return pltpu.make_async_remote_copy(
            src_ref=buf.at[g, pl.ds(0, PEERS - 1)],
            dst_ref=buf.at[g, pl.ds(0, PEERS - 1)],
            send_sem=send.at[g],
            recv_sem=recv.at[g],
            device_id={"seq": me},
            device_id_type=MESH,
        )

    def gate_group(g, _):
        g_copy(g).wait()
        bulk(recvbuf, g, ssem, rsem).wait_recv()
        chain = jnp.zeros((16, 128), F32)
        for j in range(PEERS):
            retbuf[g, j] = chain.astype(BF16)
            chain = chain * fac[g, j : j + 1] + recvbuf[g, j].astype(F32)

        def send(d, _):
            back_copy(g, lax.rem(me + d, PEERS)).start()
            return 0

        lax.fori_loop(1, PEERS, send, 0)
        retrecv[g, me] = retbuf[g, me]
        for b in range(B):
            gbuf[g, b] = dot(x[b, HALO:R], wg[g]).astype(BF16)
            for k in range(K):
                rows = slice(k * L, (k + 1) * L)
                target = dot(a3[b, k], e512[g])
                for p in range(2):
                    lanes = slice(p * 128, (p + 1) * 128)
                    mixes = []
                    for q in range(2):
                        n = 2 * p + q
                        spread = target[:, n * 128 : (n + 1) * 128] - cs_t[b, k, pl.ds(4 * g + n, 1), :]
                        mixes.append((jnp.exp2(jnp.minimum(spread, 100.0)) * sc[b, k]).astype(BF16))
                    mix = jnp.concatenate(mixes, axis=1)
                    v = vbuf[g, b, rows, lanes].astype(F32)
                    two = jnp.concatenate(
                        [jnp.where(first_half, v, 0.0), jnp.where(first_half, 0.0, v)], axis=0
                    ).astype(BF16)
                    mixbuf[g, b, rows, lanes] = dot(mix, two) + rows_s[g, 0:1, lanes] * v
        return 0

    lax.fori_loop(0, G, gate_group, 0)

    def carry_group(g, _):
        bulk(retrecv, g, tsem, usem).wait_recv()
        for b in range(B):
            halves = [
                retrecv[g, (b * 2 + h) * 8 : (b * 2 + h) * 8 + 8].reshape(128, 128) for h in range(2)
            ]
            entering = jnp.concatenate(halves, axis=1).astype(F32)
            for k in range(K):
                rows = slice(k * L, (k + 1) * L)
                if k == 0:
                    state = entering
                else:
                    state = local[g, b, k - 1] + entering * rows_b[g, b * K + k : b * K + k + 1]
                carried = dot(crow[b, k], state.astype(BF16))
                inside = dot(a2g[b, k], e256[g])
                mixture = mixbuf[g, b, rows] + inside * carried
                gated = mixture * silu(gbuf[g, b, rows].astype(F32))
                mixbuf[g, b, rows] = gated
                square = gated * gated
                sq[b, rows] = sq[b, rows] + square[:, 0:128] + square[:, 128:256]
        return 0

    lax.fori_loop(0, G, carry_group, 0)

    ones = jnp.ones((8, 256), BF16)
    for b in range(B):
        hi, mid, _ = split3(sq[b])
        terms = jnp.concatenate([hi, mid], axis=1).astype(BF16)
        ssend[b] = lax.dot_general(ones, terms, (((1,), (1,)), ((), ())), preferred_element_type=F32)

    def square_copy(d):
        return pltpu.make_async_remote_copy(
            src_ref=ssend,
            dst_ref=srecv.at[hd],
            send_sem=qsem.at[0],
            recv_sem=qsem.at[1],
            device_id={"head": lax.rem(hd + d, HEADS_AXIS)},
            device_id_type=MESH,
        )

    for d in range(1, HEADS_AXIS):
        square_copy(d).start()
    srecv[hd] = ssend[...]
    pltpu.make_async_remote_copy(
        src_ref=srecv.at[pl.ds(0, HEADS_AXIS - 1)],
        dst_ref=srecv.at[pl.ds(0, HEADS_AXIS - 1)],
        send_sem=qsem.at[0],
        recv_sem=qsem.at[1],
        device_id={"head": hd},
        device_id_type=MESH,
    ).wait_recv()
    eighth = jnp.full((16, 128), 0.125, BF16)
    for b in range(B):
        total = srecv[0, b] + srecv[1, b] + srecv[2, b] + srecv[3, b]
        inverse = lax.rsqrt(total / INNER + EPS)
        hi, mid, _ = split3(inverse)
        terms = jnp.concatenate([hi, mid], axis=0).astype(BF16)
        sq[b] = lax.dot_general(terms, eighth, (((0,), (0,)), ((), ())), preferred_element_type=F32)

    def out_copy(g):
        return pltpu.make_async_copy(
            obuf.at[g], out.at[:, :, pl.ds(pl.multiple_of(g * GC, GC), GC)], osem.at[g]
        )

    def final_group(g, _):
        base = pl.multiple_of(g * GC, GC)
        for b in range(B):
            for j in range(2):
                lanes = slice(j * 128, (j + 1) * 128)
                at = pl.ds(pl.multiple_of(base + j * 128, 128), 128)
                obuf[g, b, :, lanes] = (mixbuf[g, b, :, lanes] * sq[b] * gain[:, at]).astype(BF16)
        out_copy(g).start()
        return 0

    lax.fori_loop(0, G, final_group, 0)

    def finish(g, _):
        out_copy(g).wait()
        bulk(sendbuf, g, ssem, rsem).wait_send()
        bulk(retbuf, g, tsem, usem).wait_send()
        return 0

    lax.fori_loop(0, G, finish, 0)
    all_logs().wait_send()
    pltpu.make_async_remote_copy(
        src_ref=srecv.at[pl.ds(0, HEADS_AXIS - 1)],
        dst_ref=srecv.at[pl.ds(0, HEADS_AXIS - 1)],
        send_sem=qsem.at[0],
        recv_sem=qsem.at[1],
        device_id={"head": hd},
        device_id_type=MESH,
    ).wait_send()

    @pl.when(me < PEERS - 1)
    def _():
        halo_copy(me + 1).wait_send()


def local_program(
    tokens, gate_weight, value_weight, state_weight, step_weight, value_kernel, value_offset,
    state_kernel, state_offset, step_offset, decay_rate, skip_gain, norm_gain,
):
    anywhere = pl.BlockSpec(memory_space=pl.ANY)
    inside = pl.BlockSpec(memory_space=pltpu.VMEM)
    vm = pltpu.VMEM
    dma = pltpu.SemaphoreType.DMA
    return pl.pallas_call(
        body,
        out_shape=jax.ShapeDtypeStruct((B, T, C), BF16),
        in_specs=[anywhere] * 5 + [inside] * 8,
        out_specs=anywhere,
        scratch_shapes=[
            vm((B, R, D), BF16),
            vm((G, D, GC), BF16),
            vm((G, D, GC), BF16),
            vm((D, 2 * N), BF16),
            vm((D, H), BF16),
            vm((B, 2, R, 128), F32),
            vm((G, B, T, GC), BF16),
            vm((G, B, T, GC), BF16),
            vm((G, B, T, GC), F32),
            vm((B, K, N, L), BF16),
            vm((B, K, L, N), BF16),
            vm((B, K, L, L), F32),
            vm((B, K, L, 128), BF16),
            vm((B, K, L, 128), BF16),
            vm((B, K, L, 128), BF16),
            vm((B, K, 32, L), F32),
            vm((G, 128, 512), BF16),
            vm((G, 128, 256), BF16),
            vm((2, G, 128, 128), BF16),
            vm((G, 8, GC), F32),
            vm((G, 8, GC), F32),
            vm((G, 8, GC), F32),
            vm((40, 128), F32),
            vm((G, B, K - 1, N, GC), F32),
            vm((G, PEERS, 16, 128), BF16),
            vm((G, PEERS, 16, 128), BF16),
            vm((G, PEERS, 16, 128), BF16),
            vm((G, PEERS, 16, 128), BF16),
            vm((8, 128), F32),
            vm((PEERS, 8, 128), F32),
            vm((G, PEERS, 128), F32),
            vm((B, T, 128), F32),
            vm((B, 8, T), F32),
            vm((HEADS_AXIS, B, 8, T), F32),
            vm((G, B, T, GC), BF16),
            dma((B,)), dma((G,)), dma((G,)), dma((2,)), dma((G,)), dma((2,)),
            dma((G,)), dma((G,)), dma((G,)), dma((G,)), dma((2,)), dma((2,)),
        ],
        compiler_params=pltpu.CompilerParams(
            collective_id=0, has_side_effects=True, vmem_limit_bytes=64 * 1024 * 1024 - 65536
        ),
        name="mixer",
    )(
        tokens, gate_weight, value_weight, state_weight, step_weight, value_kernel,
        value_offset.reshape(1, C), state_kernel, state_offset.reshape(1, 2 * N),
        step_offset.reshape(1, H), decay_rate.reshape(1, H), skip_gain.reshape(1, H),
        norm_gain.reshape(1, C),
    )


def solution(mesh):
    return jax.shard_map(
        local_program,
        mesh=mesh,
        in_specs=(
            P(None, "seq", None),
            P(None, "head"),
            P(None, "head"),
            P(),
            P(None, "head"),
            P(None, "head"),
            P("head"),
            P(),
            P(),
            P("head"),
            P("head"),
            P("head"),
            P("head"),
        ),
        out_specs=P(None, "seq", "head"),
        check_vma=False,
    )
```

time: 161 us -> 80 us (0.50)
  Pallas kernels: 0 us -> 71.7 us
  matrix products: 51.6 us -> 0 us
  waiting for transfers between devices: 34.8 us -> 0 us
  starting transfers between devices: 26.5 us -> 0 us
  other arithmetic: 18.8 us -> 0 us
  local copies, waits for them, and re-layouts: 22.8 us -> 8.01 us
  blocking collectives: 4.42 us -> 0 us
    pallas_call x0 -> x1, Pallas kernels: none -> 71.7 us  [local_program(): pl.pallas_call(body, out_shape=jax.ShapeDtypeStruct((B, T, C), BF16), in_...]
    dot_general x13 -> x0, matrix products: 51.6 us -> none  [the longest x1 11.9 us: local(): jnp.einsum('btd,dc->btc', tokens, gate_weight, preferred_element_type=jnp...]
    all_to_all x4 -> x0, waiting for transfers between devices: 34.8 us -> none  [the longest x1 19.5 us: turned_blocks(): out = lax.all_to_all(out, axes[k], k, k, tiled=True)]
    all_to_all x4 -> x0, starting transfers between devices: 21.4 us -> none  [the longest x2 12 us: copy_for_each(): lax.all_to_all(jnp.broadcast_to(array[None], (count, *array.shape)), axis...]
    convert_element_type x7 -> x0, other arithmetic: 10.7 us -> none  [the longest x2 5.32 us: local(): (gated_list[block_index] * inverse[:, lower:upper, None] * norm_gain).ast...]
    ppermute x1 -> x0, starting transfers between devices: 5.1 us -> none  [shifted(): lax.ppermute(value, axis, [(source, source + steps) for source in range(l...]
    reshape x7 -> x2, local copies, waits for them, and re-layouts: 7.57 us -> 2.58 us  [the longest x1 1.29 us: local_program(): norm_gain.reshape(1, C)]
    all_to_all x1 -> x0, blocking collectives: 4.42 us -> none  [turned_blocks(): out = lax.all_to_all(out, axes[k], k, k, tiled=True)]
  transfers between devices with their start and end apart: 5 -> 0, of which waited for: 4 -> 0; matrix products, arithmetic and copies ran while one was open for 14% -> 0% of each run, Pallas kernels for 0% -> 0%
where the time goes in v1:
time: 80 us; the launch traced here: 79.7 us
  Pallas kernels  71.7 us (90%)
  local copies, waits for them, and re-layouts  8.01 us (10%)
    pallas_call x1, Pallas kernels, local_program(): pl.pallas_call(body, out_shape=jax.ShapeDtypeStruct((B, T, C), BF16), in_...  71.7 us
    unnamed x2, local copies, waits for them, and re-layouts  5.43 us

profile of v1, /device:TPU:1, one launch (start us, length us, event | category | flops | bytes accessed | tf_op | source)
XLA Modules:
  0.0 79.7 jit_solution(10981990596428349907)
XLA Ops:
  0.0 1.3 %reshape.18.value_o = f32[1,1280]{1,0:T(1,128)} reshape(f32[1280]{0:T(1024)} %param.19) | data formatting | bytes 10240 | tf_op jit(solution)/shard_map/reshape | solution.py:504
  1.3 1.3 %reshape.23.gain = f32[1,1280]{1,0:T(1,128)} reshape(f32[1280]{0:T(1024)} %param.25) | data formatting | bytes 10240 | tf_op jit(solution)/shard_map/reshape | solution.py:506
  2.6 2.0 %copy.14.step_w = bf16[2560,20]{1,0:T(8,128)(2,1)} copy(bf16[2560,20]{0,1:T(8,128)(2,1)} %param.17) | data formatting | bytes 204800 | tf_op args[4]
  4.6 71.7 %mixer.1 = bf16[2,512,1280]{2,1,0:T(8,128)(2,1)} custom-call(bf16[2,512,2560]{2,1,0:T(8,128)(2,1)} %tok.1, bf16[2560,1280]{1,0:T(8,128)(2,1)} %gate_w.1, bf16[2560,1280]{1,0:T(8,128)(2,1)} %value_w.1, bf16[2560,256]{1,0:T(8,128)(2,1)} %state_w.1, bf16[2560,20]{1,0:T(8,128)(2,1)} %copy.14.step_w, f32[4,1280]{1,0:T(4,128)} %value_k.1, ...), custom_call_target="tpu_custom_call" | custom-call | tf_op jit(solution)/shard_map/mixer/pallas_call | solution.py:454
  76.3 3.4 %copy.16 = bf16[2,512,1280]{2,1,0:T(8,128)(2,1)} copy(bf16[2,512,1280]{2,1,0:T(8,128)(2,1)} %mixer.1) | data formatting | bytes 5242880

commit v2 on v1

--- a/solution.py
+++ b/solution.py
@@ -62,12 +62,12 @@
 
 def body(
     tok, gate_w, value_w, state_w, step_w,
-    value_k, value_o, state_k, state_o, step_o, decay, skip, gain,
-    out,
-    x, wv, wg, ws, wd, cv, vbuf, gbuf, mixbuf, brow_t, crow, sc, a3, a2w, a2g, cs_t,
-    e512, e256, eh, rows_t, rows_b, rows_s, pad, local, sendbuf, recvbuf, retbuf, retrecv,
-    logsend, logrecv, fac, sq, ssend, srecv, obuf,
-    xsem, vsem, gsem, msem, osem, hsem, ssem, rsem, tsem, usem, lsem, qsem,
+    value_k, value_o, state_k, state_o, step_o, decay, skip,
+    mixbuf, inverse_out,
+    x, wv, wg, ws, wd, cv, cm, vbuf, gbuf, brow_t, crow, sc, cums, closing, a2g, cs_t,
+    e256, eh, rows_t, rows_b, rows_s, pad, local, sendbuf, recvbuf, retbuf, retrecv,
+    logsend, logrecv, fac, sq, ssend, srecv,
+    xsem, vsem, gsem, msem, hsem, ssem, rsem, tsem, usem, lsem, qsem,
 ):
     me = lax.axis_index("seq")
     hd = lax.axis_index("head")
@@ -112,7 +112,6 @@
         )
 
     for g in range(G):
-        e512[g] = spread_matrix((128, 512), 4 * g, 128)
         e256[g] = spread_matrix((128, 256), 4 * g, 64)
         for h in range(2):
             eh[h, g] = spread_matrix((128, 128), 2 * (2 * g + h), 64)
@@ -122,8 +121,6 @@
     pad[16:17, 0:H] = skip[...]
     sq[...] = jnp.zeros_like(sq)
 
-    pl.semaphore_wait(barrier, PEERS - 1 + HEADS_AXIS - 1)
-
     def halo_copy(dest):
         return pltpu.make_async_remote_copy(
             src_ref=tok.at[:, pl.ds(T - HALO, HALO)],
@@ -134,23 +131,21 @@
             device_id_type=MESH,
         )
 
-    @pl.when(me < PEERS - 1)
-    def _():
-        halo_copy(me + 1).start()
-
-    @pl.when(me == 0)
-    def _():
-        x[:, 0:HALO, :] = jnp.zeros((B, HALO, D), BF16)
-
     d_copy.wait()
     for c in x_copies:
         c.wait()
+    step_raw = [
+        lax.dot_general(
+            x[b, HALO:R], wd[...], (((1,), (1,)), ((), ())), preferred_element_type=F32
+        )
+        for b in range(B)
+    ]
     tri = lax.broadcasted_iota(jnp.int32, (L, L), 0) >= lax.broadcasted_iota(jnp.int32, (L, L), 1)
     tri16 = jnp.where(tri, 1.0, 0.0).astype(BF16)
     tri3 = jnp.concatenate([tri16, tri16, tri16], axis=1)
     logsend[...] = jnp.zeros_like(logsend)
     for b in range(B):
-        a3f = dot(x[b, HALO:R], wd[...])
+        a3f = step_raw[b]
         sq[b, :, 0:H] = a3f
         z = sq[b] + pad[0:1]
         step = jnp.maximum(z, 0.0) + jnp.log1p(jnp.exp(-jnp.abs(z)))
@@ -164,8 +159,8 @@
             cum = dot(tri3, stacked)
             last = cum[L - 1 : L]
             source = cum - log_step[k * L : (k + 1) * L]
-            a3[b, k] = packed(cum)
-            a2w[b, k] = packed(jnp.exp2(last - source))
+            cums[b, k] = cum
+            closing[b, k] = jnp.exp2(last - source)
             a2g[b, k] = packed(jnp.exp2(cum))
             cs_t[b, k] = jnp.transpose(source)[0:32]
             pad[24 + b * K + k : 25 + b * K + k] = jnp.exp2(last)
@@ -184,6 +179,17 @@
             device_id_type=MESH,
         )
 
+    pl.semaphore_wait(barrier, PEERS - 1 + HEADS_AXIS - 1)
+
+
+    @pl.when(me < PEERS - 1)
+    def _():
+        halo_copy(me + 1).start()
+
+    @pl.when(me == 0)
+    def _():
+        x[:, 0:HALO, :] = jnp.zeros((B, HALO, D), BF16)
+
     def send_log(d, _):
         log_copy(lax.rem(me + d, PEERS)).start()
         return 0
@@ -204,25 +210,6 @@
     @pl.when(me > 0)
     def _():
         halo_copy(me).wait_recv()
-
-    def convolve(b, raw, taps, offset, j):
-        cv[b, j] = raw.astype(BF16).astype(F32)
-        total = offset
-        for tap in range(TAPS):
-            total = total + taps[tap : tap + 1] * cv[b, j, pl.ds(HALO - TAPS + 1 + tap, T), :]
-        return silu(total).astype(BF16)
-
-    for b in range(B):
-        raw = dot(x[b], ws[...])
-        bmap = convolve(b, raw[:, 0:N], state_k[:, 0:N], state_o[:, 0:N], 0)
-        cmap = convolve(b, raw[:, N : 2 * N], state_k[:, N : 2 * N], state_o[:, N : 2 * N], 1)
-        for k in range(K):
-            bk = bmap[k * L : (k + 1) * L]
-            ck = cmap[k * L : (k + 1) * L]
-            crow[b, k] = ck
-            bt = jnp.transpose(bk.astype(F32)).astype(BF16)
-            brow_t[b, k] = bt
-            sc[b, k] = jnp.where(tri, dot(ck, bt), 0.0)
 
     def share_copy(g, dest):
         return pltpu.make_async_remote_copy(
@@ -244,40 +231,90 @@
             device_id_type=MESH,
         )
 
-    def value_group(g, _):
-        v_copy(g).wait()
-        base = pl.multiple_of(g * GC, GC)
-        for b in range(B):
-            raw = dot(x[b], wv[g])
+    first_half = lax.broadcasted_iota(jnp.int32, (L, 128), 1) < 64
+
+    def to_front(heads, g):
+        return pltpu.roll(heads, lax.rem(128 - 4 * g, 128), 1)
+
+    def column(heads, n):
+        return jnp.broadcast_to(heads[:, n : n + 1], (L, 128))
+
+    def value_dot(g, b):
+        for first in range(0, R, R // 2):
+            raw = dot(x[b, first : first + R // 2], wv[g]).astype(BF16).astype(F32)
             for j in range(2):
-                at = pl.ds(pl.multiple_of(base + j * 128, 128), 128)
-                vbuf[g, b, :, j * 128 : (j + 1) * 128] = convolve(
-                    b, raw[:, j * 128 : (j + 1) * 128], value_k[:, at], value_o[:, at], j
-                )
-            state = None
-            for k in range(K):
-                scale = dot(a2w[b, k], e256[g])
-                vk = vbuf[g, b, k * L : (k + 1) * L].astype(F32)
-                made = dot(brow_t[b, k], (vk * scale).astype(BF16))
-                if state is None:
-                    state = made
-                else:
-                    local[g, b, k - 1] = state
-                    state = state * rows_t[g, b * K + k : b * K + k + 1] + made
-            state = state.astype(BF16)
-            for h in range(2):
-                first = (b * 2 + h) * 8
-                sendbuf[g, first : first + 8] = state[:, h * 128 : (h + 1) * 128].reshape(8, 16, 128)
-
+                cv[b, j, first : first + R // 2] = raw[:, j * 128 : (j + 1) * 128]
+
+    def value_conv(g, b):
+        for j in range(2):
+            at = pl.ds(pl.multiple_of(g * GC + j * 128, 128), 128)
+            vbuf[g, b, :, j * 128 : (j + 1) * 128] = convolve(
+                cv, b, value_k[:, at], value_o[pl.ds(2 * g + j, 1), :], j
+            )
+
+    def value_state(g, b):
+        state = None
+        for k in range(K):
+            near = to_front(closing[b, k], g)
+            scale = jnp.concatenate(
+                [jnp.where(first_half, column(near, 2 * j), column(near, 2 * j + 1)) for j in range(2)],
+                axis=1,
+            )
+            vk = vbuf[g, b, k * L : (k + 1) * L].astype(F32)
+            made = dot(brow_t[b, k], (vk * scale).astype(BF16))
+            if state is None:
+                state = made
+            else:
+                local[g, b, k - 1] = state
+                state = state * rows_t[g, b * K + k : b * K + k + 1] + made
+        state = state.astype(BF16)
+        for h in range(2):
+            first = (b * 2 + h) * 8
+            sendbuf[g, first : first + 8] = state[:, h * 128 : (h + 1) * 128].reshape(8, 16, 128)
+
+    def send_shares(g):
         def send(d, _):
             share_copy(g, lax.rem(me + d, PEERS)).start()
             return 0
 
         lax.fori_loop(1, PEERS, send, 0)
         recvbuf[g, me] = sendbuf[g, me]
+
+    def convolve(raw, b, taps, offset, j):
+        total = offset
+        for tap in range(TAPS):
+            total = total + taps[tap : tap + 1] * raw[b, j, pl.ds(HALO - TAPS + 1 + tap, T), :]
+        return silu(total).astype(BF16)
+
+    for b in range(B):
+        for first in range(0, R, R // 2):
+            raw = dot(x[b, first : first + R // 2], ws[...]).astype(BF16).astype(F32)
+            for j in range(2):
+                cm[b, j, first : first + R // 2] = raw[:, j * 128 : (j + 1) * 128]
+    v_copy(0).wait()
+    for b in range(B):
+        value_dot(0, b)
+        bmap = convolve(cm, b, state_k[:, 0:N], state_o[0:1], 0)
+        cmap = convolve(cm, b, state_k[:, N : 2 * N], state_o[1:2], 1)
+        for k in range(K):
+            bk = bmap[k * L : (k + 1) * L]
+            ck = cmap[k * L : (k + 1) * L]
+            crow[b, k] = ck
+            bt = jnp.transpose(bk.astype(F32)).astype(BF16)
+            brow_t[b, k] = bt
+            sc[b, k] = jnp.where(tri, dot(ck, bt), 0.0)
+
+    def value_group(g, _):
+        v_copy(g).wait()
+        for b in range(B):
+            value_conv(g - 1, b)
+        for b in range(B):
+            value_dot(g, b)
+            value_state(g - 1, b)
+        send_shares(g - 1)
         return 0
 
-    lax.fori_loop(0, G, value_group, 0)
+    lax.fori_loop(1, G, value_group, 0)
 
     def all_logs():
         return pltpu.make_async_remote_copy(
@@ -289,15 +326,6 @@
             device_id_type=MESH,
         )
 
-    all_logs().wait_recv()
-    my_batch = me // 16
-    my_half = lax.rem(me // 8, 2)
-    logs = logrecv[:, pl.ds(my_batch, 1), :].reshape(PEERS, 128)
-    through = packed(jnp.exp2(logs))
-    for g in range(G):
-        fac[g] = dot(through, eh[my_half, g])
-
-    first_half = lax.broadcasted_iota(jnp.int32, (L, 128), 1) < 64
 
     def bulk(buf, g, send, recv):
         return pltpu.make_async_remote_copy(
@@ -309,8 +337,30 @@
             device_id_type=MESH,
         )
 
-    def gate_group(g, _):
-        g_copy(g).wait()
+    def gate_dot(g, b):
+        for first in range(0, T, T // 2):
+            rows = slice(first, first + T // 2)
+            gbuf[g, b, rows] = dot(x[b, HALO + first : HALO + first + T // 2], wg[g]).astype(BF16)
+
+    def within(g, b):
+        for k in range(K):
+            rows = slice(k * L, (k + 1) * L)
+            near = to_front(cums[b, k], g)
+            for p in range(2):
+                lanes = slice(p * 128, (p + 1) * 128)
+                mixes = []
+                for q in range(2):
+                    n = 2 * p + q
+                    spread = column(near, n) - cs_t[b, k, pl.ds(4 * g + n, 1), :]
+                    mixes.append((jnp.exp2(jnp.minimum(spread, 100.0)) * sc[b, k]).astype(BF16))
+                mix = jnp.concatenate(mixes, axis=1)
+                v = vbuf[g, b, rows, lanes].astype(F32)
+                two = jnp.concatenate(
+                    [jnp.where(first_half, v, 0.0), jnp.where(first_half, 0.0, v)], axis=0
+                ).astype(BF16)
+                mixbuf[g, b, rows, lanes] = dot(mix, two) + rows_s[g, 0:1, lanes] * v
+
+    def chain_share(g):
         bulk(recvbuf, g, ssem, rsem).wait_recv()
         chain = jnp.zeros((16, 128), F32)
         for j in range(PEERS):
@@ -323,27 +373,39 @@
 
         lax.fori_loop(1, PEERS, send, 0)
         retrecv[g, me] = retbuf[g, me]
+
+    g_copy(0).wait()
+    for b in range(B):
+        value_conv(G - 1, b)
+    for b in range(B):
+        gate_dot(0, b)
+        value_state(G - 1, b)
+    send_shares(G - 1)
+
+    all_logs().wait_recv()
+    my_batch = me // 16
+    my_half = lax.rem(me // 8, 2)
+    logs = logrecv[:, pl.ds(my_batch, 1), :].reshape(PEERS, 128)
+    through = packed(jnp.exp2(logs))
+    for g in range(G):
+        fac[g] = dot(through, eh[my_half, g])
+
+    def gate_group(g, _):
+        g_copy(g).wait()
         for b in range(B):
-            gbuf[g, b] = dot(x[b, HALO:R], wg[g]).astype(BF16)
-            for k in range(K):
-                rows = slice(k * L, (k + 1) * L)
-                target = dot(a3[b, k], e512[g])
-                for p in range(2):
-                    lanes = slice(p * 128, (p + 1) * 128)
-                    mixes = []
-                    for q in range(2):
-                        n = 2 * p + q
-                        spread = target[:, n * 128 : (n + 1) * 128] - cs_t[b, k, pl.ds(4 * g + n, 1), :]
-                        mixes.append((jnp.exp2(jnp.minimum(spread, 100.0)) * sc[b, k]).astype(BF16))
-                    mix = jnp.concatenate(mixes, axis=1)
-                    v = vbuf[g, b, rows, lanes].astype(F32)
-                    two = jnp.concatenate(
-                        [jnp.where(first_half, v, 0.0), jnp.where(first_half, 0.0, v)], axis=0
-                    ).astype(BF16)
-                    mixbuf[g, b, rows, lanes] = dot(mix, two) + rows_s[g, 0:1, lanes] * v
+            gate_dot(g, b)
+            within(g - 1, b)
         return 0
 
-    lax.fori_loop(0, G, gate_group, 0)
+    lax.fori_loop(1, G, gate_group, 0)
+
+    def chain_group(g, _):
+        chain_share(g)
+        return 0
+
+    lax.fori_loop(0, G, chain_group, 0)
+    for b in range(B):
+        within(G - 1, b)
 
     def carry_group(g, _):
         bulk(retrecv, g, tsem, usem).wait_recv()
@@ -402,27 +464,9 @@
         inverse = lax.rsqrt(total / INNER + EPS)
         hi, mid, _ = split3(inverse)
         terms = jnp.concatenate([hi, mid], axis=0).astype(BF16)
-        sq[b] = lax.dot_general(terms, eighth, (((0,), (0,)), ((), ())), preferred_element_type=F32)
-
-    def out_copy(g):
-        return pltpu.make_async_copy(
-            obuf.at[g], out.at[:, :, pl.ds(pl.multiple_of(g * GC, GC), GC)], osem.at[g]
-        )
-
-    def final_group(g, _):
-        base = pl.multiple_of(g * GC, GC)
-        for b in range(B):
-            for j in range(2):
-                lanes = slice(j * 128, (j + 1) * 128)
-                at = pl.ds(pl.multiple_of(base + j * 128, 128), 128)
-                obuf[g, b, :, lanes] = (mixbuf[g, b, :, lanes] * sq[b] * gain[:, at]).astype(BF16)
-        out_copy(g).start()
-        return 0
-
-    lax.fori_loop(0, G, final_group, 0)
+        inverse_out[b] = lax.dot_general(terms, eighth, (((0,), (0,)), ((), ())), preferred_element_type=F32)
 
     def finish(g, _):
-        out_copy(g).wait()
         bulk(sendbuf, g, ssem, rsem).wait_send()
         bulk(retbuf, g, tsem, usem).wait_send()
         return 0
@@ -443,6 +487,25 @@
         halo_copy(me + 1).wait_send()
 
 
+def scale(gated, inverse, gain, out, obuf, sem):
+    copies = []
+    for g in range(G):
+        for b in range(B):
+            for j in range(2):
+                lanes = slice(j * 128, (j + 1) * 128)
+                obuf[g, b, :, lanes] = (
+                    gated[g, b, :, lanes] * inverse[b] * gain[2 * g + j : 2 * g + j + 1]
+                ).astype(BF16)
+            copies.append(
+                pltpu.make_async_copy(
+                    obuf.at[g, b], out.at[b, :, pl.ds(g * GC, GC)], sem.at[g, b]
+                )
+            )
+            copies[-1].start()
+    for c in copies:
+        c.wait()
+
+
 def local_program(
     tokens, gate_weight, value_weight, state_weight, step_weight, value_kernel, value_offset,
     state_kernel, state_offset, step_offset, decay_rate, skip_gain, norm_gain,
@@ -451,29 +514,28 @@
     inside = pl.BlockSpec(memory_space=pltpu.VMEM)
     vm = pltpu.VMEM
     dma = pltpu.SemaphoreType.DMA
-    return pl.pallas_call(
+    gated, inverse = pl.pallas_call(
         body,
-        out_shape=jax.ShapeDtypeStruct((B, T, C), BF16),
-        in_specs=[anywhere] * 5 + [inside] * 8,
-        out_specs=anywhere,
+        out_shape=(vm((G, B, T, GC), F32), vm((B, T, 128), F32)),
+        in_specs=[anywhere] * 5 + [inside] * 7,
+        out_specs=(inside, inside),
         scratch_shapes=[
             vm((B, R, D), BF16),
             vm((G, D, GC), BF16),
             vm((G, D, GC), BF16),
             vm((D, 2 * N), BF16),
-            vm((D, H), BF16),
+            vm((H, D), BF16),
+            vm((B, 2, R, 128), F32),
             vm((B, 2, R, 128), F32),
             vm((G, B, T, GC), BF16),
             vm((G, B, T, GC), BF16),
-            vm((G, B, T, GC), F32),
             vm((B, K, N, L), BF16),
             vm((B, K, L, N), BF16),
             vm((B, K, L, L), F32),
-            vm((B, K, L, 128), BF16),
-            vm((B, K, L, 128), BF16),
+            vm((B, K, L, 128), F32),
+            vm((B, K, L, 128), F32),
             vm((B, K, L, 128), BF16),
             vm((B, K, 32, L), F32),
-            vm((G, 128, 512), BF16),
             vm((G, 128, 256), BF16),
             vm((2, G, 128, 128), BF16),
             vm((G, 8, GC), F32),
@@ -491,20 +553,27 @@
             vm((B, T, 128), F32),
             vm((B, 8, T), F32),
             vm((HEADS_AXIS, B, 8, T), F32),
-            vm((G, B, T, GC), BF16),
-            dma((B,)), dma((G,)), dma((G,)), dma((2,)), dma((G,)), dma((2,)),
+            dma((B,)), dma((G,)), dma((G,)), dma((2,)), dma((2,)),
             dma((G,)), dma((G,)), dma((G,)), dma((G,)), dma((2,)), dma((2,)),
         ],
         compiler_params=pltpu.CompilerParams(
-            collective_id=0, has_side_effects=True, vmem_limit_bytes=64 * 1024 * 1024 - 65536
+            collective_id=0, has_side_effects=True, vmem_limit_bytes=50 * 1024 * 1024
         ),
         name="mixer",
     )(
-        tokens, gate_weight, value_weight, state_weight, step_weight, value_kernel,
-        value_offset.reshape(1, C), state_kernel, state_offset.reshape(1, 2 * N),
+        tokens, gate_weight, value_weight, state_weight, step_weight.T, value_kernel,
+        value_offset.reshape(C // 128, 128), state_kernel, state_offset.reshape(2, N),
         step_offset.reshape(1, H), decay_rate.reshape(1, H), skip_gain.reshape(1, H),
-        norm_gain.reshape(1, C),
     )
+    return pl.pallas_call(
+        scale,
+        out_shape=jax.ShapeDtypeStruct((B, T, C), BF16),
+        in_specs=[inside] * 3,
+        out_specs=anywhere,
+        scratch_shapes=[vm((G, B, T, GC), BF16), dma((G, B))],
+        compiler_params=pltpu.CompilerParams(vmem_limit_bytes=8 * 1024 * 1024),
+        name="scale",
+    )(gated, inverse, norm_gain.reshape(C // 128, 128))
 
 
 def solution(mesh):

time: 80 us -> 56.4 us (0.70)
  Pallas kernels: 71.7 us -> 56.2 us
  local copies, waits for them, and re-layouts: 8.01 us -> 0.01 us
    pallas_call x1 -> x2, Pallas kernels: 71.7 us -> 56.2 us  [the longest x1 54.6 us: local_program(): pl.pallas_call(body, out_shape=(vm((G, B, T, GC), F32), vm((B, T, 128), F...]
    unnamed x2, local copies, waits for them, and re-layouts: 5.43 us -> 0.01 us
    reshape x2 -> x0, local copies, waits for them, and re-layouts: 2.58 us -> none  [the longest x1 1.29 us: local_program(): norm_gain.reshape(1, C)]
where the time goes in v2:
time: 56.4 us; the launch traced here: 56.3 us
  Pallas kernels  56.2 us (100%)
    pallas_call x1, Pallas kernels, local_program(): pl.pallas_call(body, out_shape=(vm((G, B, T, GC), F32), vm((B, T, 128), F...  54.6 us
    pallas_call x1, Pallas kernels, local_program(): pl.pallas_call(scale, out_shape=jax.ShapeDtypeStruct((B, T, C), BF16), in...  1.63 us

profile of v2, /device:TPU:1, one launch (start us, length us, event | category | flops | bytes accessed | tf_op | source)
XLA Modules:
  0.0 56.3 jit_solution(4066783992202604282)
XLA Ops:
  0.0 0.0 copy-start
  0.0 54.6 %mixer.1 = (f32[5,2,512,256]{3,2,1,0:T(8,128)S(1)}, f32[2,512,128]{2,1,0:T(8,128)S(1)}) custom-call(bf16[2,512,2560]{2,1,0:T(8,128)(2,1)} %tok.1, bf16[2560,1280]{1,0:T(8,128)(2,1)} %gate_w.1, bf16[2560,1280]{1,0:T(8,128)(2,1)} %value_w.1, bf16[2560,256]{1,0:T(8,128)(2,1)} %state_w.1, bf16[20,2560]{1,0:T(8,128)(2,1)} %bitcast.8, f32[4,1280]{1,0:T(4,128)} %value_k.1, ...), custom_call_target="tpu_custom_call" | custom-call | tf_op jit(solution)/shard_map/mixer/pallas_call | solution.py:517
  54.6 0.0 copy-done
  54.6 1.6 %scale.1 = bf16[2,512,1280]{2,1,0:T(8,128)(2,1)} custom-call(f32[5,2,512,256]{3,2,1,0:T(8,128)S(1)} %get-tuple-element.7.gated, f32[2,512,128]{2,1,0:T(8,128)S(1)} %get-tuple-element.8.inverse, f32[10,128]{1,0:T(8,128)S(1)} %bitcast.7), custom_call_target="tpu_custom_call" | custom-call | tf_op jit(solution)/shard_map/scale/pallas_call | solution.py:568
Async XLA Ops:
  0.0 54.6 %copy-start = (f32[1280]{0:T(1024)S(1)}, f32[1280]{0:T(1024)}, u32[]{:S(2)}) copy-start(f32[1280]{0:T(1024)} %param.25) | copy-start | bytes 15364

commit v3 on v2

--- a/solution.py
+++ b/solution.py
@@ -62,12 +62,13 @@
 
 def body(
     tok, gate_w, value_w, state_w, step_w,
+    value_k_in, value_o_in, state_k_in, state_o_in, step_o_in, decay_in, skip_in,
+    mixbuf, inverse_out,
     value_k, value_o, state_k, state_o, step_o, decay, skip,
-    mixbuf, inverse_out,
     x, wv, wg, ws, wd, cv, cm, vbuf, gbuf, brow_t, crow, sc, cums, closing, a2g, cs_t,
     e256, eh, rows_t, rows_b, rows_s, pad, local, sendbuf, recvbuf, retbuf, retrecv,
     logsend, logrecv, fac, sq, ssend, srecv,
-    xsem, vsem, gsem, msem, hsem, ssem, rsem, tsem, usem, lsem, qsem,
+    xsem, vsem, gsem, msem, psem, hsem, ssem, rsem, tsem, usem, lsem, qsem,
 ):
     me = lax.axis_index("seq")
     hd = lax.axis_index("head")
@@ -88,14 +89,22 @@
             gate_w.at[:, pl.ds(pl.multiple_of(g * GC, GC), GC)], wg.at[g], gsem.at[g]
         )
 
+    small = [
+        pltpu.make_async_copy(src, dst, psem.at[i])
+        for i, (src, dst) in enumerate(
+            (
+                (step_o_in, step_o), (decay_in, decay), (skip_in, skip), (state_k_in, state_k),
+                (state_o_in, state_o), (value_k_in, value_k), (value_o_in, value_o),
+            )
+        )
+    ]
     d_copy.start()
     for c in x_copies:
         c.start()
+    for c in small:
+        c.start()
     s_copy.start()
-    for g in range(G):
-        v_copy(g).start()
-    for g in range(G):
-        g_copy(g).start()
+    v_copy(0).start()
 
     barrier = pltpu.get_barrier_semaphore()
 
@@ -116,10 +125,8 @@
         for h in range(2):
             eh[h, g] = spread_matrix((128, 128), 2 * (2 * g + h), 64)
     pad[...] = jnp.zeros_like(pad)
-    pad[0:1, 0:H] = step_o[...]
-    pad[8:9, 0:H] = decay[...]
-    pad[16:17, 0:H] = skip[...]
     sq[...] = jnp.zeros_like(sq)
+    logsend[...] = jnp.zeros_like(logsend)
 
     def halo_copy(dest):
         return pltpu.make_async_remote_copy(
@@ -132,21 +139,38 @@
         )
 
     d_copy.wait()
-    for c in x_copies:
+    for b in range(B):
+        x_copies[b].wait()
+        for first in range(0, T, T // 2):
+            sq[b, first : first + T // 2, 0:H] = lax.dot_general(
+                x[b, HALO + first : HALO + first + T // 2], wd[...], (((1,), (1,)), ((), ())),
+                preferred_element_type=F32,
+            )
+    for g in range(1, G):
+        v_copy(g).start()
+    for c in small:
         c.wait()
-    step_raw = [
-        lax.dot_general(
-            x[b, HALO:R], wd[...], (((1,), (1,)), ((), ())), preferred_element_type=F32
-        )
-        for b in range(B)
-    ]
+    pad[0:1, 0:H] = step_o[...]
+    pad[8:9, 0:H] = decay[...]
+    pad[16:17, 0:H] = skip[...]
+
+    pl.semaphore_wait(barrier, PEERS - 1 + HEADS_AXIS - 1)
+
+    @pl.when(me < PEERS - 1)
+    def _():
+        halo_copy(me + 1).start()
+
+    @pl.when(me == 0)
+    def _():
+        x[:, 0:HALO, :] = jnp.zeros((B, HALO, D), BF16)
+
+    s_copy.wait()
+    v_copy(0).wait()
     tri = lax.broadcasted_iota(jnp.int32, (L, L), 0) >= lax.broadcasted_iota(jnp.int32, (L, L), 1)
     tri16 = jnp.where(tri, 1.0, 0.0).astype(BF16)
     tri3 = jnp.concatenate([tri16, tri16, tri16], axis=1)
-    logsend[...] = jnp.zeros_like(logsend)
-    for b in range(B):
-        a3f = step_raw[b]
-        sq[b, :, 0:H] = a3f
+
+    def step_sizes(b):
         z = sq[b] + pad[0:1]
         step = jnp.maximum(z, 0.0) + jnp.log1p(jnp.exp(-jnp.abs(z)))
         decayed = step * (pad[8:9] * (-LOG2E))
@@ -167,7 +191,25 @@
             pad[32 + b * K + k : 33 + b * K + k] = jnp.exp2(before)
             before = before + last
         logsend[b : b + 1] = before
-    sq[...] = jnp.zeros_like(sq)
+        sq[b] = jnp.zeros_like(sq[b])
+
+    def main_dot(b, weights, into):
+        for first in range(HALO, R, T // 2):
+            raw = dot(x[b, first : first + T // 2], weights).astype(BF16).astype(F32)
+            for j in range(2):
+                into[b, j, first : first + T // 2] = raw[:, j * 128 : (j + 1) * 128]
+
+    def halo_dot(weights, into):
+        raw = dot(x[:, 0:HALO].reshape(B * HALO, D), weights).astype(BF16).astype(F32)
+        for b in range(B):
+            for j in range(2):
+                into[b, j, 0:HALO] = raw[b * HALO : (b + 1) * HALO, j * 128 : (j + 1) * 128]
+
+    for b in range(B):
+        main_dot(b, ws[...], cm)
+    for b in range(B):
+        step_sizes(b)
+        main_dot(b, wv[0], cv)
 
     def log_copy(dest):
         return pltpu.make_async_remote_copy(
@@ -179,37 +221,13 @@
             device_id_type=MESH,
         )
 
-    pl.semaphore_wait(barrier, PEERS - 1 + HEADS_AXIS - 1)
-
-
-    @pl.when(me < PEERS - 1)
-    def _():
-        halo_copy(me + 1).start()
-
-    @pl.when(me == 0)
-    def _():
-        x[:, 0:HALO, :] = jnp.zeros((B, HALO, D), BF16)
-
-    def send_log(d, _):
-        log_copy(lax.rem(me + d, PEERS)).start()
-        return 0
-
-    lax.fori_loop(1, PEERS, send_log, 0)
-    logrecv[me] = logsend[...]
-
-    rt = packed(pad[24:32])
-    rb = packed(pad[32:40])
-    rs = packed(pad[16:24])
-    for g in range(G):
-        rows_t[g] = dot(rt, e256[g])
-        rows_b[g] = dot(rb, e256[g])
-        rows_s[g] = dot(rs, e256[g])
-
-    s_copy.wait()
-
     @pl.when(me > 0)
     def _():
         halo_copy(me).wait_recv()
+
+    for d in range(1, PEERS):
+        log_copy(lax.rem(me + d, PEERS)).start()
+    logrecv[me] = logsend[...]
 
     def share_copy(g, dest):
         return pltpu.make_async_remote_copy(
@@ -273,11 +291,8 @@
             sendbuf[g, first : first + 8] = state[:, h * 128 : (h + 1) * 128].reshape(8, 16, 128)
 
     def send_shares(g):
-        def send(d, _):
+        for d in range(1, PEERS):
             share_copy(g, lax.rem(me + d, PEERS)).start()
-            return 0
-
-        lax.fori_loop(1, PEERS, send, 0)
         recvbuf[g, me] = sendbuf[g, me]
 
     def convolve(raw, b, taps, offset, j):
@@ -285,47 +300,6 @@
         for tap in range(TAPS):
             total = total + taps[tap : tap + 1] * raw[b, j, pl.ds(HALO - TAPS + 1 + tap, T), :]
         return silu(total).astype(BF16)
-
-    for b in range(B):
-        for first in range(0, R, R // 2):
-            raw = dot(x[b, first : first + R // 2], ws[...]).astype(BF16).astype(F32)
-            for j in range(2):
-                cm[b, j, first : first + R // 2] = raw[:, j * 128 : (j + 1) * 128]
-    v_copy(0).wait()
-    for b in range(B):
-        value_dot(0, b)
-        bmap = convolve(cm, b, state_k[:, 0:N], state_o[0:1], 0)
-        cmap = convolve(cm, b, state_k[:, N : 2 * N], state_o[1:2], 1)
-        for k in range(K):
-            bk = bmap[k * L : (k + 1) * L]
-            ck = cmap[k * L : (k + 1) * L]
-            crow[b, k] = ck
-            bt = jnp.transpose(bk.astype(F32)).astype(BF16)
-            brow_t[b, k] = bt
-            sc[b, k] = jnp.where(tri, dot(ck, bt), 0.0)
-
-    def value_group(g, _):
-        v_copy(g).wait()
-        for b in range(B):
-            value_conv(g - 1, b)
-        for b in range(B):
-            value_dot(g, b)
-            value_state(g - 1, b)
-        send_shares(g - 1)
-        return 0
-
-    lax.fori_loop(1, G, value_group, 0)
-
-    def all_logs():
-        return pltpu.make_async_remote_copy(
-            src_ref=logrecv.at[pl.ds(0, PEERS - 1)],
-            dst_ref=logrecv.at[pl.ds(0, PEERS - 1)],
-            send_sem=lsem.at[0],
-            recv_sem=lsem.at[1],
-            device_id={"seq": me},
-            device_id_type=MESH,
-        )
-
 
     def bulk(buf, g, send, recv):
         return pltpu.make_async_remote_copy(
@@ -361,26 +335,86 @@
                 mixbuf[g, b, rows, lanes] = dot(mix, two) + rows_s[g, 0:1, lanes] * v
 
     def chain_share(g):
-        bulk(recvbuf, g, ssem, rsem).wait_recv()
         chain = jnp.zeros((16, 128), F32)
         for j in range(PEERS):
             retbuf[g, j] = chain.astype(BF16)
             chain = chain * fac[g, j : j + 1] + recvbuf[g, j].astype(F32)
 
-        def send(d, _):
+        for d in range(1, PEERS):
             back_copy(g, lax.rem(me + d, PEERS)).start()
-            return 0
-
-        lax.fori_loop(1, PEERS, send, 0)
         retrecv[g, me] = retbuf[g, me]
 
-    g_copy(0).wait()
-    for b in range(B):
-        value_conv(G - 1, b)
-    for b in range(B):
-        gate_dot(0, b)
-        value_state(G - 1, b)
-    send_shares(G - 1)
+    def carry(g, b):
+        halves = [
+            retrecv[g, (b * 2 + h) * 8 : (b * 2 + h) * 8 + 8].reshape(128, 128) for h in range(2)
+        ]
+        entering = jnp.concatenate(halves, axis=1).astype(F32)
+        for k in range(K):
+            rows = slice(k * L, (k + 1) * L)
+            if k == 0:
+                state = entering
+            else:
+                state = local[g, b, k - 1] + entering * rows_b[g, b * K + k : b * K + k + 1]
+            carried = dot(crow[b, k], state.astype(BF16))
+            inside = dot(a2g[b, k], e256[g])
+            mixture = mixbuf[g, b, rows] + inside * carried
+            gated = mixture * silu(gbuf[g, b, rows].astype(F32))
+            mixbuf[g, b, rows] = gated
+            square = gated * gated
+            sq[b, rows] = sq[b, rows] + square[:, 0:128] + square[:, 128:256]
+
+    v_copy(1).wait()
+    halo_dot(ws[...], cm)
+    halo_dot(wv[0], cv)
+    rt = packed(pad[24:32])
+    rb = packed(pad[32:40])
+    rs = packed(pad[16:24])
+    for g in range(G):
+        rows_t[g] = dot(rt, e256[g])
+        rows_b[g] = dot(rb, e256[g])
+        rows_s[g] = dot(rs, e256[g])
+    for b in range(B):
+        bmap = convolve(cm, b, state_k[:, 0:N], state_o[0:1], 0)
+        cmap = convolve(cm, b, state_k[:, N : 2 * N], state_o[1:2], 1)
+        for k in range(K):
+            crow[b, k] = cmap[k * L : (k + 1) * L]
+            brow_t[b, k] = jnp.transpose(bmap[k * L : (k + 1) * L].astype(F32)).astype(BF16)
+        value_conv(0, b)
+    for b in range(B):
+        value_dot(1, b)
+        for k in range(K):
+            sc[b, k] = jnp.where(tri, dot(crow[b, k], brow_t[b, k]), 0.0)
+        value_state(0, b)
+    for g in range(G):
+        g_copy(g).start()
+
+    def value_group(g, _):
+        v_copy(g).wait()
+        send_shares(g - 2)
+        for b in range(B):
+            value_conv(g - 1, b)
+        for b in range(B):
+            value_dot(g, b)
+            value_state(g - 1, b)
+        return 0
+
+    lax.fori_loop(2, G, value_group, 0)
+
+    def all_logs():
+        return pltpu.make_async_remote_copy(
+            src_ref=logrecv.at[pl.ds(0, PEERS - 1)],
+            dst_ref=logrecv.at[pl.ds(0, PEERS - 1)],
+            send_sem=lsem.at[0],
+            recv_sem=lsem.at[1],
+            device_id={"seq": me},
+            device_id_type=MESH,
+        )
+
+    def arrived(g):
+        bulk(recvbuf, g, ssem, rsem).wait_recv()
+
+    def returned(g):
+        bulk(retrecv, g, tsem, usem).wait_recv()
 
     all_logs().wait_recv()
     my_batch = me // 16
@@ -390,46 +424,57 @@
     for g in range(G):
         fac[g] = dot(through, eh[my_half, g])
 
-    def gate_group(g, _):
-        g_copy(g).wait()
-        for b in range(B):
-            gate_dot(g, b)
-            within(g - 1, b)
-        return 0
-
-    lax.fori_loop(1, G, gate_group, 0)
-
-    def chain_group(g, _):
-        chain_share(g)
-        return 0
-
-    lax.fori_loop(0, G, chain_group, 0)
-    for b in range(B):
-        within(G - 1, b)
-
-    def carry_group(g, _):
-        bulk(retrecv, g, tsem, usem).wait_recv()
-        for b in range(B):
-            halves = [
-                retrecv[g, (b * 2 + h) * 8 : (b * 2 + h) * 8 + 8].reshape(128, 128) for h in range(2)
-            ]
-            entering = jnp.concatenate(halves, axis=1).astype(F32)
-            for k in range(K):
-                rows = slice(k * L, (k + 1) * L)
-                if k == 0:
-                    state = entering
-                else:
-                    state = local[g, b, k - 1] + entering * rows_b[g, b * K + k : b * K + k + 1]
-                carried = dot(crow[b, k], state.astype(BF16))
-                inside = dot(a2g[b, k], e256[g])
-                mixture = mixbuf[g, b, rows] + inside * carried
-                gated = mixture * silu(gbuf[g, b, rows].astype(F32))
-                mixbuf[g, b, rows] = gated
-                square = gated * gated
-                sq[b, rows] = sq[b, rows] + square[:, 0:128] + square[:, 128:256]
-        return 0
-
-    lax.fori_loop(0, G, carry_group, 0)
+    g_copy(0).wait()
+    arrived(0)
+    send_shares(3)
+    chain_share(0)
+    for b in range(B):
+        value_conv(4, b)
+    for b in range(B):
+        gate_dot(0, b)
+        value_state(4, b)
+
+    g_copy(1).wait()
+    arrived(1)
+    send_shares(4)
+    chain_share(1)
+    for b in range(B):
+        gate_dot(1, b)
+        within(b, 0)
+        within(b, 1)
+
+    g_copy(2).wait()
+    arrived(2)
+    arrived(3)
+    chain_share(2)
+    chain_share(3)
+    for b in range(B):
+        gate_dot(2, b)
+        within(2 + b, 0)
+        within(2 + b, 1)
+
+    g_copy(3).wait()
+    arrived(4)
+    returned(0)
+    chain_share(4)
+    for b in range(B):
+        carry(0, b)
+        gate_dot(3, b)
+        within(4, b)
+
+    g_copy(4).wait()
+    returned(1)
+    returned(2)
+    for b in range(B):
+        carry(1 + b, 0)
+        gate_dot(4, b)
+        carry(1 + b, 1)
+
+    returned(3)
+    returned(4)
+    for b in range(B):
+        carry(3, b)
+        carry(4, b)
 
     ones = jnp.ones((8, 256), BF16)
     for b in range(B):
@@ -517,9 +562,16 @@
     gated, inverse = pl.pallas_call(
         body,
         out_shape=(vm((G, B, T, GC), F32), vm((B, T, 128), F32)),
-        in_specs=[anywhere] * 5 + [inside] * 7,
+        in_specs=[anywhere] * 12,
         out_specs=(inside, inside),
         scratch_shapes=[
+            vm((TAPS, C), F32),
+            vm((C // 128, 128), F32),
+            vm((TAPS, 2 * N), F32),
+            vm((2, N), F32),
+            vm((1, H), F32),
+            vm((1, H), F32),
+            vm((1, H), F32),
             vm((B, R, D), BF16),
             vm((G, D, GC), BF16),
             vm((G, D, GC), BF16),
@@ -553,7 +605,7 @@
             vm((B, T, 128), F32),
             vm((B, 8, T), F32),
             vm((HEADS_AXIS, B, 8, T), F32),
-            dma((B,)), dma((G,)), dma((G,)), dma((2,)), dma((2,)),
+            dma((B,)), dma((G,)), dma((G,)), dma((2,)), dma((7,)), dma((2,)),
             dma((G,)), dma((G,)), dma((G,)), dma((G,)), dma((2,)), dma((2,)),
         ],
         compiler_params=pltpu.CompilerParams(

time: 56.4 us -> 44.4 us (0.79)
  Pallas kernels: 56.2 us -> 44.1 us
    pallas_call x1, Pallas kernels: 54.6 us -> 42.5 us  [local_program(): pl.pallas_call(body, out_shape=(vm((G, B, T, GC), F32), vm((B, T, 128), F...]
where the time goes in v3:
time: 44.4 us; the launch traced here: 44.3 us
  Pallas kernels  44.1 us (99%)
    pallas_call x1, Pallas kernels, local_program(): pl.pallas_call(body, out_shape=(vm((G, B, T, GC), F32), vm((B, T, 128), F...  42.5 us
    pallas_call x1, Pallas kernels, local_program(): pl.pallas_call(scale, out_shape=jax.ShapeDtypeStruct((B, T, C), BF16), in...  1.63 us

profile of v3, /device:TPU:1, one launch (start us, length us, event | category | flops | bytes accessed | tf_op | source)
XLA Modules:
  0.0 44.3 jit_solution(13177390446875192673)
XLA Ops:
  0.0 0.0 copy-start
  0.0 42.5 %mixer.1 = (f32[5,2,512,256]{3,2,1,0:T(8,128)S(1)}, f32[2,512,128]{2,1,0:T(8,128)S(1)}) custom-call(bf16[2,512,2560]{2,1,0:T(8,128)(2,1)} %tok.1, bf16[2560,1280]{1,0:T(8,128)(2,1)} %gate_w.1, bf16[2560,1280]{1,0:T(8,128)(2,1)} %value_w.1, bf16[2560,256]{1,0:T(8,128)(2,1)} %state_w.1, bf16[20,2560]{1,0:T(8,128)(2,1)} %bitcast.8, f32[4,1280]{1,0:T(4,128)} %value_k_in.1, ...), custom_call_target="tpu_custom_call" | custom-call | tf_op jit(solution)/shard_map/mixer/pallas_call | solution.py:562
  42.5 0.0 copy-done
  42.5 1.6 %scale.1 = bf16[2,512,1280]{2,1,0:T(8,128)(2,1)} custom-call(f32[5,2,512,256]{3,2,1,0:T(8,128)S(1)} %get-tuple-element.7.gated, f32[2,512,128]{2,1,0:T(8,128)S(1)} %get-tuple-element.8.inverse, f32[10,128]{1,0:T(8,128)S(1)} %bitcast.7), custom_call_target="tpu_custom_call" | custom-call | tf_op jit(solution)/shard_map/scale/pallas_call | solution.py:620
Async XLA Ops:
  0.0 42.5 %copy-start = (f32[1280]{0:T(1024)S(1)}, f32[1280]{0:T(1024)}, u32[]{:S(2)}) copy-start(f32[1280]{0:T(1024)} %param.25) | copy-start | bytes 15364

commit v4 on v3

--- a/solution.py
+++ b/solution.py
@@ -26,7 +26,9 @@
 HALO = 16
 R = T + HALO
 TAPS = 4
+LUMPS = ((0, 2), (2, 1), (3, 1), (4, 1), (5, 1))
 PEERS = 32
+CHIPS = 16
 HEADS_AXIS = 4
 INNER = 5120
 
@@ -66,12 +68,16 @@
     mixbuf, inverse_out,
     value_k, value_o, state_k, state_o, step_o, decay, skip,
     x, wv, wg, ws, wd, cv, cm, vbuf, gbuf, brow_t, crow, sc, cums, closing, a2g, cs_t,
-    e256, eh, rows_t, rows_b, rows_s, pad, local, sendbuf, recvbuf, retbuf, retrecv,
-    logsend, logrecv, fac, sq, ssend, srecv,
-    xsem, vsem, gsem, msem, psem, hsem, ssem, rsem, tsem, usem, lsem, qsem,
+    e256, eh, rows_t, rows_b, rows_s, pad, local, pairsend, pairrecv, logs_out, logs_in, rows_c, sendbuf, recvbuf, retbuf, retrecv,
+    fac, sq, ssend, srecv,
+    xsem, vsem, gsem, msem, psem, hsem,
+    wsem, zsem, lsem, ssem, rsem, tsem, usem, qsem,
 ):
     me = lax.axis_index("seq")
     hd = lax.axis_index("head")
+    core = lax.rem(me, 2)
+    chip = lax.div(me, 2)
+    partner = me + 1 - 2 * core
 
     x_copies = [
         pltpu.make_async_copy(tok.at[b], x.at[b, pl.ds(HALO, T)], xsem.at[b]) for b in range(B)
@@ -126,7 +132,8 @@
             eh[h, g] = spread_matrix((128, 128), 2 * (2 * g + h), 64)
     pad[...] = jnp.zeros_like(pad)
     sq[...] = jnp.zeros_like(sq)
-    logsend[...] = jnp.zeros_like(logsend)
+    retbuf[:, 0] = jnp.zeros((CHIPS, 16, 128), BF16)
+    logs_out[...] = jnp.zeros_like(logs_out)
 
     def halo_copy(dest):
         return pltpu.make_async_remote_copy(
@@ -190,7 +197,7 @@
             pad[24 + b * K + k : 25 + b * K + k] = jnp.exp2(last)
             pad[32 + b * K + k : 33 + b * K + k] = jnp.exp2(before)
             before = before + last
-        logsend[b : b + 1] = before
+        logs_out[b : b + 1] = before
         sq[b] = jnp.zeros_like(sq[b])
 
     def main_dot(b, weights, into):
@@ -211,40 +218,52 @@
         step_sizes(b)
         main_dot(b, wv[0], cv)
 
-    def log_copy(dest):
+    def log_copy():
         return pltpu.make_async_remote_copy(
-            src_ref=logsend,
-            dst_ref=logrecv.at[me],
+            src_ref=logs_out,
+            dst_ref=logs_in,
             send_sem=lsem.at[0],
             recv_sem=lsem.at[1],
-            device_id={"seq": dest},
+            device_id={"seq": partner},
             device_id_type=MESH,
         )
+
+    log_copy().start()
 
     @pl.when(me > 0)
     def _():
         halo_copy(me).wait_recv()
 
-    for d in range(1, PEERS):
-        log_copy(lax.rem(me + d, PEERS)).start()
-    logrecv[me] = logsend[...]
-
-    def share_copy(g, dest):
+    def tiles(buf, lump, at):
+        first, count = LUMPS[lump]
+        return buf.at[at, pl.ds(first, count)]
+
+    def pair_copy(g):
         return pltpu.make_async_remote_copy(
-            src_ref=sendbuf.at[g, dest],
-            dst_ref=recvbuf.at[g, me],
-            send_sem=ssem.at[g],
-            recv_sem=rsem.at[g],
-            device_id={"seq": dest},
+            src_ref=pairsend.at[g],
+            dst_ref=pairrecv.at[g],
+            send_sem=wsem.at[g],
+            recv_sem=zsem.at[g],
+            device_id={"seq": partner},
             device_id_type=MESH,
         )
 
-    def back_copy(g, dest):
+    def share_copy(lump, to_chip):
         return pltpu.make_async_remote_copy(
-            src_ref=retbuf.at[g, dest],
-            dst_ref=retrecv.at[g, me],
-            send_sem=tsem.at[g],
-            recv_sem=usem.at[g],
+            src_ref=tiles(sendbuf, lump, to_chip),
+            dst_ref=tiles(recvbuf, lump, chip),
+            send_sem=ssem.at[lump],
+            recv_sem=rsem.at[lump],
+            device_id={"seq": 2 * to_chip + core},
+            device_id_type=MESH,
+        )
+
+    def back_copy(lump, dest):
+        return pltpu.make_async_remote_copy(
+            src_ref=tiles(retbuf, lump, lax.div(dest, 2)),
+            dst_ref=tiles(retrecv, lump, core * CHIPS + chip),
+            send_sem=tsem.at[lump],
+            recv_sem=usem.at[lump],
             device_id={"seq": dest},
             device_id_type=MESH,
         )
@@ -285,15 +304,40 @@
             else:
                 local[g, b, k - 1] = state
                 state = state * rows_t[g, b * K + k : b * K + k + 1] + made
-        state = state.astype(BF16)
+        pairsend[g, b] = state.astype(BF16)
+
+    def chip_decays():
+        log_copy().wait_recv()
+        second_core = core == 1
+        early = jnp.where(second_core, logs_in[...], logs_out[...])
+        late = jnp.where(second_core, logs_out[...], logs_in[...])
+        both = jnp.exp2(early + late)
+        both = jnp.where(second_core, both[1:2], both[0:1])
+        sendbuf[:, 0] = jnp.broadcast_to(
+            packed(jnp.broadcast_to(both, (16, 128)))[None], (CHIPS, 16, 128)
+        )
+        late = jnp.where(second_core, late[1:2], late[0:1])
+        none = jnp.zeros((1, 128), F32)
+        pad[40:41] = jnp.where(second_core, none, late)
+        pad[41:42] = jnp.where(second_core, late, none)
+        pad[42:44] = jnp.where(second_core, early[0:2], jnp.zeros((2, 128), F32))
+        factors = packed(jnp.exp2(pad[40:48]))
+        for g in range(G):
+            rows_c[g] = dot(factors, e256[g])
+
+    def send_shares(lump):
+        pair_copy(lump).wait_recv()
+        whole = (
+            rows_c[lump, 0:1] * pairsend[lump, core].astype(F32)
+            + rows_c[lump, 1:2] * pairrecv[lump, core].astype(F32)
+        ).astype(BF16)
         for h in range(2):
-            first = (b * 2 + h) * 8
-            sendbuf[g, first : first + 8] = state[:, h * 128 : (h + 1) * 128].reshape(8, 16, 128)
-
-    def send_shares(g):
-        for d in range(1, PEERS):
-            share_copy(g, lax.rem(me + d, PEERS)).start()
-        recvbuf[g, me] = sendbuf[g, me]
+            sendbuf[h * 8 : h * 8 + 8, lump + 1] = whole[:, h * 128 : (h + 1) * 128].reshape(8, 16, 128)
+        for d in range(1, CHIPS):
+            ahead = chip + d
+            share_copy(lump, jnp.where(ahead < CHIPS, ahead, ahead - CHIPS)).start()
+        first, count = LUMPS[lump]
+        recvbuf[chip, first : first + count] = sendbuf[chip, first : first + count]
 
     def convolve(raw, b, taps, offset, j):
         total = offset
@@ -301,12 +345,12 @@
             total = total + taps[tap : tap + 1] * raw[b, j, pl.ds(HALO - TAPS + 1 + tap, T), :]
         return silu(total).astype(BF16)
 
-    def bulk(buf, g, send, recv):
+    def bulk(buf, lump, count, send, recv):
         return pltpu.make_async_remote_copy(
-            src_ref=buf.at[g, pl.ds(0, PEERS - 1)],
-            dst_ref=buf.at[g, pl.ds(0, PEERS - 1)],
-            send_sem=send.at[g],
-            recv_sem=recv.at[g],
+            src_ref=tiles(buf, lump, pl.ds(0, count)),
+            dst_ref=tiles(buf, lump, pl.ds(0, count)),
+            send_sem=send.at[lump],
+            recv_sem=recv.at[lump],
             device_id={"seq": me},
             device_id_type=MESH,
         )
@@ -326,7 +370,7 @@
                 for q in range(2):
                     n = 2 * p + q
                     spread = column(near, n) - cs_t[b, k, pl.ds(4 * g + n, 1), :]
-                    mixes.append((jnp.exp2(jnp.minimum(spread, 100.0)) * sc[b, k]).astype(BF16))
+                    mixes.append(jnp.exp2(jnp.minimum(spread, 100.0)).astype(BF16) * sc[b, k])
                 mix = jnp.concatenate(mixes, axis=1)
                 v = vbuf[g, b, rows, lanes].astype(F32)
                 two = jnp.concatenate(
@@ -334,21 +378,23 @@
                 ).astype(BF16)
                 mixbuf[g, b, rows, lanes] = dot(mix, two) + rows_s[g, 0:1, lanes] * v
 
-    def chain_share(g):
+    def chain_share(lump):
+        first, count = LUMPS[lump]
         chain = jnp.zeros((16, 128), F32)
-        for j in range(PEERS):
-            retbuf[g, j] = chain.astype(BF16)
-            chain = chain * fac[g, j : j + 1] + recvbuf[g, j].astype(F32)
-
+        for j in range(CHIPS):
+            retbuf[j, lump + 1] = chain.astype(BF16)
+            chain = chain * fac[lump, j] + recvbuf[j, lump + 1].astype(F32)
         for d in range(1, PEERS):
-            back_copy(g, lax.rem(me + d, PEERS)).start()
-        retrecv[g, me] = retbuf[g, me]
+            ahead = me + d
+            back_copy(lump, jnp.where(ahead < PEERS, ahead, ahead - PEERS)).start()
+        retrecv[core * CHIPS + chip, first : first + count] = retbuf[chip, first : first + count]
 
     def carry(g, b):
         halves = [
-            retrecv[g, (b * 2 + h) * 8 : (b * 2 + h) * 8 + 8].reshape(128, 128) for h in range(2)
+            retrecv[(b * 2 + h) * 8 : (b * 2 + h) * 8 + 8, g + 1].reshape(128, 128) for h in range(2)
         ]
-        entering = jnp.concatenate(halves, axis=1).astype(F32)
+        entering = rows_c[g, 2 + b : 3 + b] * jnp.concatenate(halves, axis=1).astype(F32)
+        entering = entering + core.astype(F32) * pairrecv[g, b].astype(F32)
         for k in range(K):
             rows = slice(k * L, (k + 1) * L)
             if k == 0:
@@ -383,51 +429,33 @@
     for b in range(B):
         value_dot(1, b)
         for k in range(K):
-            sc[b, k] = jnp.where(tri, dot(crow[b, k], brow_t[b, k]), 0.0)
+            sc[b, k] = jnp.where(tri, dot(crow[b, k], brow_t[b, k]), 0.0).astype(BF16)
         value_state(0, b)
     for g in range(G):
         g_copy(g).start()
 
-    def value_group(g, _):
+    for g in range(2, G):
         v_copy(g).wait()
-        send_shares(g - 2)
+        pair_copy(g - 2).start()
+        if g == 3:
+            chip_decays()
+        if g > 2:
+            send_shares(g - 3)
         for b in range(B):
             value_conv(g - 1, b)
         for b in range(B):
             value_dot(g, b)
             value_state(g - 1, b)
-        return 0
-
-    lax.fori_loop(2, G, value_group, 0)
-
-    def all_logs():
-        return pltpu.make_async_remote_copy(
-            src_ref=logrecv.at[pl.ds(0, PEERS - 1)],
-            dst_ref=logrecv.at[pl.ds(0, PEERS - 1)],
-            send_sem=lsem.at[0],
-            recv_sem=lsem.at[1],
-            device_id={"seq": me},
-            device_id_type=MESH,
-        )
-
-    def arrived(g):
-        bulk(recvbuf, g, ssem, rsem).wait_recv()
-
-    def returned(g):
-        bulk(retrecv, g, tsem, usem).wait_recv()
-
-    all_logs().wait_recv()
-    my_batch = me // 16
-    my_half = lax.rem(me // 8, 2)
-    logs = logrecv[:, pl.ds(my_batch, 1), :].reshape(PEERS, 128)
-    through = packed(jnp.exp2(logs))
-    for g in range(G):
-        fac[g] = dot(through, eh[my_half, g])
+
+    def arrived(lump):
+        bulk(recvbuf, lump, CHIPS - 1, ssem, rsem).wait_recv()
+
+    def returned(lump):
+        bulk(retrecv, lump, PEERS - 1, tsem, usem).wait_recv()
 
     g_copy(0).wait()
-    arrived(0)
-    send_shares(3)
-    chain_share(0)
+    pair_copy(3).start()
+    send_shares(2)
     for b in range(B):
         value_conv(4, b)
     for b in range(B):
@@ -435,40 +463,50 @@
         value_state(4, b)
 
     g_copy(1).wait()
+    pair_copy(4).start()
+    send_shares(3)
+    arrived(0)
+    my_half = lax.div(chip, 8)
+    through = recvbuf[:, 0].reshape(CHIPS * 16, 128)
+    for g in range(G):
+        fac[g] = dot(through, eh[my_half, g]).reshape(CHIPS, 16, 128)
+    chain_share(0)
+    for b in range(B):
+        gate_dot(1, b)
+        within(0, b)
+
+    send_shares(4)
     arrived(1)
-    send_shares(4)
+    arrived(2)
     chain_share(1)
-    for b in range(B):
-        gate_dot(1, b)
-        within(b, 0)
-        within(b, 1)
-
+    chain_share(2)
     g_copy(2).wait()
-    arrived(2)
+    for b in range(B):
+        gate_dot(2, b)
+        within(1, b)
+
+    g_copy(3).wait()
     arrived(3)
-    chain_share(2)
     chain_share(3)
     for b in range(B):
-        gate_dot(2, b)
-        within(2 + b, 0)
-        within(2 + b, 1)
-
-    g_copy(3).wait()
+        gate_dot(3, b)
+        within(2, b)
+
+    g_copy(4).wait()
     arrived(4)
+    chain_share(4)
+    for b in range(B):
+        gate_dot(4, b)
+        within(3, b)
+        within(4, b)
+
     returned(0)
-    chain_share(4)
-    for b in range(B):
-        carry(0, b)
-        gate_dot(3, b)
-        within(4, b)
-
-    g_copy(4).wait()
     returned(1)
     returned(2)
     for b in range(B):
-        carry(1 + b, 0)
-        gate_dot(4, b)
-        carry(1 + b, 1)
+        carry(0, b)
+        carry(1, b)
+        carry(2, b)
 
     returned(3)
     returned(4)
@@ -511,13 +549,11 @@
         terms = jnp.concatenate([hi, mid], axis=0).astype(BF16)
         inverse_out[b] = lax.dot_general(terms, eighth, (((0,), (0,)), ((), ())), preferred_element_type=F32)
 
-    def finish(g, _):
-        bulk(sendbuf, g, ssem, rsem).wait_send()
-        bulk(retbuf, g, tsem, usem).wait_send()
-        return 0
-
-    lax.fori_loop(0, G, finish, 0)
-    all_logs().wait_send()
+    log_copy().wait_send()
+    for lump in range(G):
+        pair_copy(lump).wait_send()
+        bulk(sendbuf, lump, CHIPS - 1, ssem, rsem).wait_send()
+        bulk(retrecv, lump, PEERS - 1, tsem, usem).wait_send()
     pltpu.make_async_remote_copy(
         src_ref=srecv.at[pl.ds(0, HEADS_AXIS - 1)],
         dst_ref=srecv.at[pl.ds(0, HEADS_AXIS - 1)],
@@ -534,16 +570,21 @@
 
 def scale(gated, inverse, gain, out, obuf, sem):
     copies = []
-    for g in range(G):
-        for b in range(B):
-            for j in range(2):
-                lanes = slice(j * 128, (j + 1) * 128)
-                obuf[g, b, :, lanes] = (
-                    gated[g, b, :, lanes] * inverse[b] * gain[2 * g + j : 2 * g + j + 1]
-                ).astype(BF16)
+    for b in range(B):
+        for k in range(K):
+            rows = slice(k * L, (k + 1) * L)
+            factor = inverse[b, rows]
+            for g in range(G):
+                for j in range(2):
+                    first = g * GC + j * 128
+                    obuf[b, rows, first : first + 128] = (
+                        gated[g, b, rows, j * 128 : (j + 1) * 128]
+                        * factor
+                        * gain[2 * g + j : 2 * g + j + 1]
+                    ).astype(BF16)
             copies.append(
                 pltpu.make_async_copy(
-                    obuf.at[g, b], out.at[b, :, pl.ds(g * GC, GC)], sem.at[g, b]
+                    obuf.at[b, pl.ds(k * L, L)], out.at[b, pl.ds(k * L, L)], sem.at[b, k]
                 )
             )
             copies[-1].start()
@@ -583,7 +624,7 @@
             vm((G, B, T, GC), BF16),
             vm((B, K, N, L), BF16),
             vm((B, K, L, N), BF16),
-            vm((B, K, L, L), F32),
+            vm((B, K, L, L), BF16),
             vm((B, K, L, 128), F32),
             vm((B, K, L, 128), F32),
             vm((B, K, L, 128), BF16),
@@ -593,20 +634,24 @@
             vm((G, 8, GC), F32),
             vm((G, 8, GC), F32),
             vm((G, 8, GC), F32),
-            vm((40, 128), F32),
+            vm((48, 128), F32),
             vm((G, B, K - 1, N, GC), F32),
-            vm((G, PEERS, 16, 128), BF16),
-            vm((G, PEERS, 16, 128), BF16),
-            vm((G, PEERS, 16, 128), BF16),
-            vm((G, PEERS, 16, 128), BF16),
+            vm((G, B, N, GC), BF16),
+            vm((G, B, N, GC), BF16),
             vm((8, 128), F32),
-            vm((PEERS, 8, 128), F32),
-            vm((G, PEERS, 128), F32),
+            vm((8, 128), F32),
+            vm((G, 8, GC), F32),
+            vm((CHIPS, G + 1, 16, 128), BF16),
+            vm((CHIPS, G + 1, 16, 128), BF16),
+            vm((CHIPS, G + 1, 16, 128), BF16),
+            vm((PEERS, G + 1, 16, 128), BF16),
+            vm((G, CHIPS, 16, 128), F32),
             vm((B, T, 128), F32),
             vm((B, 8, T), F32),
             vm((HEADS_AXIS, B, 8, T), F32),
             dma((B,)), dma((G,)), dma((G,)), dma((2,)), dma((7,)), dma((2,)),
-            dma((G,)), dma((G,)), dma((G,)), dma((G,)), dma((2,)), dma((2,)),
+            dma((G,)), dma((G,)), dma((2,)),
+            dma((G,)), dma((G,)), dma((G,)), dma((G,)), dma((2,)),
         ],
         compiler_params=pltpu.CompilerParams(
             collective_id=0, has_side_effects=True, vmem_limit_bytes=50 * 1024 * 1024
@@ -622,7 +667,7 @@
         out_shape=jax.ShapeDtypeStruct((B, T, C), BF16),
         in_specs=[inside] * 3,
         out_specs=anywhere,
-        scratch_shapes=[vm((G, B, T, GC), BF16), dma((G, B))],
+        scratch_shapes=[vm((B, T, C), BF16), dma((B, K))],
         compiler_params=pltpu.CompilerParams(vmem_limit_bytes=8 * 1024 * 1024),
         name="scale",
     )(gated, inverse, norm_gain.reshape(C // 128, 128))

time: 44.4 us -> 45.2 us (1.018)
  Pallas kernels: 44.1 us -> 45 us
    pallas_call x1, Pallas kernels: 42.5 us -> 43.3 us  [local_program(): pl.pallas_call(body, out_shape=(vm((G, B, T, GC), F32), vm((B, T, 128), F...]
where the time goes in v4:
time: 45.2 us; the launch traced here: 45.1 us
  Pallas kernels  45 us (100%)
    pallas_call x1, Pallas kernels, local_program(): pl.pallas_call(body, out_shape=(vm((G, B, T, GC), F32), vm((B, T, 128), F...  43.3 us
    pallas_call x1, Pallas kernels, local_program(): pl.pallas_call(scale, out_shape=jax.ShapeDtypeStruct((B, T, C), BF16), in...  1.62 us

profile of v4, /device:TPU:1, one launch (start us, length us, event | category | flops | bytes accessed | tf_op | source)
XLA Modules:
  0.0 45.1 jit_solution(5713934109879401658)
XLA Ops:
  0.0 0.0 copy-start
  0.0 43.3 %mixer.1 = (f32[5,2,512,256]{3,2,1,0:T(8,128)S(1)}, f32[2,512,128]{2,1,0:T(8,128)S(1)}) custom-call(bf16[2,512,2560]{2,1,0:T(8,128)(2,1)} %tok.1, bf16[2560,1280]{1,0:T(8,128)(2,1)} %gate_w.1, bf16[2560,1280]{1,0:T(8,128)(2,1)} %value_w.1, bf16[2560,256]{1,0:T(8,128)(2,1)} %state_w.1, bf16[20,2560]{1,0:T(8,128)(2,1)} %bitcast.8, f32[4,1280]{1,0:T(4,128)} %value_k_in.1, ...), custom_call_target="tpu_custom_call" | custom-call | tf_op jit(solution)/shard_map/mixer/pallas_call | solution.py:603
  43.4 0.0 copy-done
  43.4 1.6 %scale.1 = bf16[2,512,1280]{2,1,0:T(8,128)(2,1)} custom-call(f32[5,2,512,256]{3,2,1,0:T(8,128)S(1)} %get-tuple-element.7.gated, f32[2,512,128]{2,1,0:T(8,128)S(1)} %get-tuple-element.8.inverse, f32[10,128]{1,0:T(8,128)S(1)} %bitcast.7), custom_call_target="tpu_custom_call" | custom-call | tf_op jit(solution)/shard_map/scale/pallas_call | solution.py:665
Async XLA Ops:
  0.0 43.4 %copy-start = (f32[1280]{0:T(1024)S(1)}, f32[1280]{0:T(1024)}, u32[]{:S(2)}) copy-start(f32[1280]{0:T(1024)} %param.25) | copy-start | bytes 15364

commit v5 on v3

--- a/solution.py
+++ b/solution.py
@@ -26,6 +26,7 @@
 HALO = 16
 R = T + HALO
 TAPS = 4
+LUMPS = ((0, 2), (2, 1), (3, 1), (4, 1), (5, 1))
 PEERS = 32
 HEADS_AXIS = 4
 INNER = 5120
@@ -67,8 +68,8 @@
     value_k, value_o, state_k, state_o, step_o, decay, skip,
     x, wv, wg, ws, wd, cv, cm, vbuf, gbuf, brow_t, crow, sc, cums, closing, a2g, cs_t,
     e256, eh, rows_t, rows_b, rows_s, pad, local, sendbuf, recvbuf, retbuf, retrecv,
-    logsend, logrecv, fac, sq, ssend, srecv,
-    xsem, vsem, gsem, msem, psem, hsem, ssem, rsem, tsem, usem, lsem, qsem,
+    fac, sq, ssend, srecv,
+    xsem, vsem, gsem, msem, psem, hsem, ssem, rsem, tsem, usem, qsem,
 ):
     me = lax.axis_index("seq")
     hd = lax.axis_index("head")
@@ -126,7 +127,7 @@
             eh[h, g] = spread_matrix((128, 128), 2 * (2 * g + h), 64)
     pad[...] = jnp.zeros_like(pad)
     sq[...] = jnp.zeros_like(sq)
-    logsend[...] = jnp.zeros_like(logsend)
+    retbuf[:, 0] = jnp.zeros((PEERS, 16, 128), BF16)
 
     def halo_copy(dest):
         return pltpu.make_async_remote_copy(
@@ -190,7 +191,8 @@
             pad[24 + b * K + k : 25 + b * K + k] = jnp.exp2(last)
             pad[32 + b * K + k : 33 + b * K + k] = jnp.exp2(before)
             before = before + last
-        logsend[b : b + 1] = before
+        whole = packed(jnp.broadcast_to(jnp.exp2(before), (16, 128)))
+        sendbuf[16 * b : 16 * b + 16, 0] = jnp.broadcast_to(whole[None], (16, 16, 128))
         sq[b] = jnp.zeros_like(sq[b])
 
     def main_dot(b, weights, into):
@@ -211,40 +213,34 @@
         step_sizes(b)
         main_dot(b, wv[0], cv)
 
-    def log_copy(dest):
-        return pltpu.make_async_remote_copy(
-            src_ref=logsend,
-            dst_ref=logrecv.at[me],
-            send_sem=lsem.at[0],
-            recv_sem=lsem.at[1],
-            device_id={"seq": dest},
-            device_id_type=MESH,
-        )
-
     @pl.when(me > 0)
     def _():
         halo_copy(me).wait_recv()
 
-    for d in range(1, PEERS):
-        log_copy(lax.rem(me + d, PEERS)).start()
-    logrecv[me] = logsend[...]
-
-    def share_copy(g, dest):
+    def peer(d):
+        ahead = me + d
+        return jnp.where(ahead < PEERS, ahead, ahead - PEERS)
+
+    def tiles(buf, lump, at):
+        first, count = LUMPS[lump]
+        return buf.at[at, pl.ds(first, count)]
+
+    def share_copy(lump, dest):
         return pltpu.make_async_remote_copy(
-            src_ref=sendbuf.at[g, dest],
-            dst_ref=recvbuf.at[g, me],
-            send_sem=ssem.at[g],
-            recv_sem=rsem.at[g],
+            src_ref=tiles(sendbuf, lump, dest),
+            dst_ref=tiles(recvbuf, lump, me),
+            send_sem=ssem.at[lump],
+            recv_sem=rsem.at[lump],
             device_id={"seq": dest},
             device_id_type=MESH,
         )
 
-    def back_copy(g, dest):
+    def back_copy(lump, dest):
         return pltpu.make_async_remote_copy(
-            src_ref=retbuf.at[g, dest],
-            dst_ref=retrecv.at[g, me],
-            send_sem=tsem.at[g],
-            recv_sem=usem.at[g],
+            src_ref=tiles(retbuf, lump, dest),
+            dst_ref=tiles(retrecv, lump, me),
+            send_sem=tsem.at[lump],
+            recv_sem=usem.at[lump],
             device_id={"seq": dest},
             device_id_type=MESH,
         )
@@ -288,12 +284,13 @@
         state = state.astype(BF16)
         for h in range(2):
             first = (b * 2 + h) * 8
-            sendbuf[g, first : first + 8] = state[:, h * 128 : (h + 1) * 128].reshape(8, 16, 128)
-
-    def send_shares(g):
+            sendbuf[first : first + 8, g + 1] = state[:, h * 128 : (h + 1) * 128].reshape(8, 16, 128)
+
+    def send_shares(lump):
         for d in range(1, PEERS):
-            share_copy(g, lax.rem(me + d, PEERS)).start()
-        recvbuf[g, me] = sendbuf[g, me]
+            share_copy(lump, peer(d)).start()
+        first, count = LUMPS[lump]
+        recvbuf[me, first : first + count] = sendbuf[me, first : first + count]
 
     def convolve(raw, b, taps, offset, j):
         total = offset
@@ -301,12 +298,12 @@
             total = total + taps[tap : tap + 1] * raw[b, j, pl.ds(HALO - TAPS + 1 + tap, T), :]
         return silu(total).astype(BF16)
 
-    def bulk(buf, g, send, recv):
+    def bulk(buf, lump, send, recv):
         return pltpu.make_async_remote_copy(
-            src_ref=buf.at[g, pl.ds(0, PEERS - 1)],
-            dst_ref=buf.at[g, pl.ds(0, PEERS - 1)],
-            send_sem=send.at[g],
-            recv_sem=recv.at[g],
+            src_ref=tiles(buf, lump, pl.ds(0, PEERS - 1)),
+            dst_ref=tiles(buf, lump, pl.ds(0, PEERS - 1)),
+            send_sem=send.at[lump],
+            recv_sem=recv.at[lump],
             device_id={"seq": me},
             device_id_type=MESH,
         )
@@ -326,7 +323,7 @@
                 for q in range(2):
                     n = 2 * p + q
                     spread = column(near, n) - cs_t[b, k, pl.ds(4 * g + n, 1), :]
-                    mixes.append((jnp.exp2(jnp.minimum(spread, 100.0)) * sc[b, k]).astype(BF16))
+                    mixes.append(jnp.exp2(jnp.minimum(spread, 100.0)).astype(BF16) * sc[b, k])
                 mix = jnp.concatenate(mixes, axis=1)
                 v = vbuf[g, b, rows, lanes].astype(F32)
                 two = jnp.concatenate(
@@ -334,19 +331,21 @@
                 ).astype(BF16)
                 mixbuf[g, b, rows, lanes] = dot(mix, two) + rows_s[g, 0:1, lanes] * v
 
-    def chain_share(g):
-        chain = jnp.zeros((16, 128), F32)
-        for j in range(PEERS):
-            retbuf[g, j] = chain.astype(BF16)
-            chain = chain * fac[g, j : j + 1] + recvbuf[g, j].astype(F32)
+    def chain_share(lump):
+        first, count = LUMPS[lump]
+        for tile in range(max(first, 1), first + count):
+            chain = jnp.zeros((16, 128), F32)
+            for j in range(PEERS):
+                retbuf[j, tile] = chain.astype(BF16)
+                chain = chain * fac[tile - 1, j] + recvbuf[j, tile].astype(F32)
 
         for d in range(1, PEERS):
-            back_copy(g, lax.rem(me + d, PEERS)).start()
-        retrecv[g, me] = retbuf[g, me]
+            back_copy(lump, peer(d)).start()
+        retrecv[me, first : first + count] = retbuf[me, first : first + count]
 
     def carry(g, b):
         halves = [
-            retrecv[g, (b * 2 + h) * 8 : (b * 2 + h) * 8 + 8].reshape(128, 128) for h in range(2)
+            retrecv[(b * 2 + h) * 8 : (b * 2 + h) * 8 + 8, g + 1].reshape(128, 128) for h in range(2)
         ]
         entering = jnp.concatenate(halves, axis=1).astype(F32)
         for k in range(K):
@@ -383,12 +382,12 @@
     for b in range(B):
         value_dot(1, b)
         for k in range(K):
-            sc[b, k] = jnp.where(tri, dot(crow[b, k], brow_t[b, k]), 0.0)
+            sc[b, k] = jnp.where(tri, dot(crow[b, k], brow_t[b, k]), 0.0).astype(BF16)
         value_state(0, b)
     for g in range(G):
         g_copy(g).start()
 
-    def value_group(g, _):
+    for g in range(2, G):
         v_copy(g).wait()
         send_shares(g - 2)
         for b in range(B):
@@ -396,37 +395,20 @@
         for b in range(B):
             value_dot(g, b)
             value_state(g - 1, b)
-        return 0
-
-    lax.fori_loop(2, G, value_group, 0)
-
-    def all_logs():
-        return pltpu.make_async_remote_copy(
-            src_ref=logrecv.at[pl.ds(0, PEERS - 1)],
-            dst_ref=logrecv.at[pl.ds(0, PEERS - 1)],
-            send_sem=lsem.at[0],
-            recv_sem=lsem.at[1],
-            device_id={"seq": me},
-            device_id_type=MESH,
-        )
-
-    def arrived(g):
-        bulk(recvbuf, g, ssem, rsem).wait_recv()
-
-    def returned(g):
-        bulk(retrecv, g, tsem, usem).wait_recv()
-
-    all_logs().wait_recv()
-    my_batch = me // 16
-    my_half = lax.rem(me // 8, 2)
-    logs = logrecv[:, pl.ds(my_batch, 1), :].reshape(PEERS, 128)
-    through = packed(jnp.exp2(logs))
-    for g in range(G):
-        fac[g] = dot(through, eh[my_half, g])
+
+    def arrived(lump):
+        bulk(recvbuf, lump, ssem, rsem).wait_recv()
+
+    def returned(lump):
+        bulk(retrecv, lump, tsem, usem).wait_recv()
 
     g_copy(0).wait()
     arrived(0)
     send_shares(3)
+    my_half = lax.rem(me // 8, 2)
+    through = recvbuf[:, 0].reshape(PEERS * 16, 128)
+    for g in range(G):
+        fac[g] = dot(through, eh[my_half, g]).reshape(PEERS, 16, 128)
     chain_share(0)
     for b in range(B):
         value_conv(4, b)
@@ -511,13 +493,9 @@
         terms = jnp.concatenate([hi, mid], axis=0).astype(BF16)
         inverse_out[b] = lax.dot_general(terms, eighth, (((0,), (0,)), ((), ())), preferred_element_type=F32)
 
-    def finish(g, _):
-        bulk(sendbuf, g, ssem, rsem).wait_send()
-        bulk(retbuf, g, tsem, usem).wait_send()
-        return 0
-
-    lax.fori_loop(0, G, finish, 0)
-    all_logs().wait_send()
+    for lump in range(G):
+        bulk(sendbuf, lump, ssem, rsem).wait_send()
+        bulk(retbuf, lump, tsem, usem).wait_send()
     pltpu.make_async_remote_copy(
         src_ref=srecv.at[pl.ds(0, HEADS_AXIS - 1)],
         dst_ref=srecv.at[pl.ds(0, HEADS_AXIS - 1)],
@@ -534,16 +512,21 @@
 
 def scale(gated, inverse, gain, out, obuf, sem):
     copies = []
-    for g in range(G):
-        for b in range(B):
-            for j in range(2):
-                lanes = slice(j * 128, (j + 1) * 128)
-                obuf[g, b, :, lanes] = (
-                    gated[g, b, :, lanes] * inverse[b] * gain[2 * g + j : 2 * g + j + 1]
-                ).astype(BF16)
+    for b in range(B):
+        for k in range(K):
+            rows = slice(k * L, (k + 1) * L)
+            factor = inverse[b, rows]
+            for g in range(G):
+                for j in range(2):
+                    first = g * GC + j * 128
+                    obuf[b, rows, first : first + 128] = (
+                        gated[g, b, rows, j * 128 : (j + 1) * 128]
+                        * factor
+                        * gain[2 * g + j : 2 * g + j + 1]
+                    ).astype(BF16)
             copies.append(
                 pltpu.make_async_copy(
-                    obuf.at[g, b], out.at[b, :, pl.ds(g * GC, GC)], sem.at[g, b]
+                    obuf.at[b, pl.ds(k * L, L)], out.at[b, pl.ds(k * L, L)], sem.at[b, k]
                 )
             )
             copies[-1].start()
@@ -583,7 +566,7 @@
             vm((G, B, T, GC), BF16),
             vm((B, K, N, L), BF16),
             vm((B, K, L, N), BF16),
-            vm((B, K, L, L), F32),
+            vm((B, K, L, L), BF16),
             vm((B, K, L, 128), F32),
             vm((B, K, L, 128), F32),
             vm((B, K, L, 128), BF16),
@@ -595,18 +578,16 @@
             vm((G, 8, GC), F32),
             vm((40, 128), F32),
             vm((G, B, K - 1, N, GC), F32),
-            vm((G, PEERS, 16, 128), BF16),
-            vm((G, PEERS, 16, 128), BF16),
-            vm((G, PEERS, 16, 128), BF16),
-            vm((G, PEERS, 16, 128), BF16),
-            vm((8, 128), F32),
-            vm((PEERS, 8, 128), F32),
-            vm((G, PEERS, 128), F32),
+            vm((PEERS, G + 1, 16, 128), BF16),
+            vm((PEERS, G + 1, 16, 128), BF16),
+            vm((PEERS, G + 1, 16, 128), BF16),
+            vm((PEERS, G + 1, 16, 128), BF16),
+            vm((G, PEERS, 16, 128), F32),
             vm((B, T, 128), F32),
             vm((B, 8, T), F32),
             vm((HEADS_AXIS, B, 8, T), F32),
             dma((B,)), dma((G,)), dma((G,)), dma((2,)), dma((7,)), dma((2,)),
-            dma((G,)), dma((G,)), dma((G,)), dma((G,)), dma((2,)), dma((2,)),
+            dma((G,)), dma((G,)), dma((G,)), dma((G,)), dma((2,)),
         ],
         compiler_params=pltpu.CompilerParams(
             collective_id=0, has_side_effects=True, vmem_limit_bytes=50 * 1024 * 1024
@@ -622,7 +603,7 @@
         out_shape=jax.ShapeDtypeStruct((B, T, C), BF16),
         in_specs=[inside] * 3,
         out_specs=anywhere,
-        scratch_shapes=[vm((G, B, T, GC), BF16), dma((G, B))],
+        scratch_shapes=[vm((B, T, C), BF16), dma((B, K))],
         compiler_params=pltpu.CompilerParams(vmem_limit_bytes=8 * 1024 * 1024),
         name="scale",
     )(gated, inverse, norm_gain.reshape(C // 128, 128))

time: 44.4 us -> 44.9 us (1.011)
  Pallas kernels: 44.1 us -> 44.6 us
where the time goes in v5:
time: 44.9 us; the launch traced here: 44.8 us
  Pallas kernels  44.6 us (99%)
    pallas_call x1, Pallas kernels, local_program(): pl.pallas_call(body, out_shape=(vm((G, B, T, GC), F32), vm((B, T, 128), F...  43 us
    pallas_call x1, Pallas kernels, local_program(): pl.pallas_call(scale, out_shape=jax.ShapeDtypeStruct((B, T, C), BF16), in...  1.62 us

profile of v5, /device:TPU:1, one launch (start us, length us, event | category | flops | bytes accessed | tf_op | source)
XLA Modules:
  0.0 44.8 jit_solution(4174678523178165571)
XLA Ops:
  0.0 0.0 copy-start
  0.0 43.0 %mixer.1 = (f32[5,2,512,256]{3,2,1,0:T(8,128)S(1)}, f32[2,512,128]{2,1,0:T(8,128)S(1)}) custom-call(bf16[2,512,2560]{2,1,0:T(8,128)(2,1)} %tok.1, bf16[2560,1280]{1,0:T(8,128)(2,1)} %gate_w.1, bf16[2560,1280]{1,0:T(8,128)(2,1)} %value_w.1, bf16[2560,256]{1,0:T(8,128)(2,1)} %state_w.1, bf16[20,2560]{1,0:T(8,128)(2,1)} %bitcast.8, f32[4,1280]{1,0:T(4,128)} %value_k_in.1, ...), custom_call_target="tpu_custom_call" | custom-call | tf_op jit(solution)/shard_map/mixer/pallas_call | solution.py:545
  43.0 0.0 copy-done
  43.0 1.6 %scale.1 = bf16[2,512,1280]{2,1,0:T(8,128)(2,1)} custom-call(f32[5,2,512,256]{3,2,1,0:T(8,128)S(1)} %get-tuple-element.7.gated, f32[2,512,128]{2,1,0:T(8,128)S(1)} %get-tuple-element.8.inverse, f32[10,128]{1,0:T(8,128)S(1)} %bitcast.7), custom_call_target="tpu_custom_call" | custom-call | tf_op jit(solution)/shard_map/scale/pallas_call | solution.py:601
Async XLA Ops:
  0.0 43.0 %copy-start = (f32[1280]{0:T(1024)S(1)}, f32[1280]{0:T(1024)}, u32[]{:S(2)}) copy-start(f32[1280]{0:T(1024)} %param.25) | copy-start | bytes 15364
